TPU v7x, 256 devices: a 2x2x32 block of a 4x8x32 slice. The times are simulated.
256 devices in a mesh: member: 4 (over y, x), lat: 64 (over z, core).
Axes of the slice: x: 2, y: 2, z: 32, core: 2. Of those that a mesh axis runs over, the one named last changes fastest.
The devices are a block of a 4x8x32 slice.
Arguments:
- field: bfloat16 [1536, 1440, 256], P(('member', 'lat')), parts along dimension 0, may hold values from -3000 to 3000
- gain: float32 [256], replicated, may hold values from 0.1 to 1.9
- slot_wave: int32 [384], replicated, may hold values from 0 to 384, as said below
- legendre: bfloat16 [384, 384, 384], P('lat'), may hold values from -0.3125 to 0.3125
- mixing: bfloat16 [384, 2, 256, 256], P('lat'), may hold values from -0.25 to 0.25
Outputs:
- result: bfloat16 [1536, 1440, 256], P(('member', 'lat')), parts along dimension 0
There are 4 independent parts, one for each index of `member`. A program takes and returns all parts, laid end to end along the dimension named above; an argument that names none is the same for every part. Nothing has to cross between parts.
Inputs may be any that keep to these rules, and one draw needn't show every extreme that they name: `slot_wave`: each wavenumber 0 to 383 stands in exactly one slot and every other slot holds 384; slots 2k and 2k+1 of one lat index hold wavenumbers adding up to (4k+2)64 - 1 where both are below 384.
All inputs are finite; a program needn't handle non-finite values.
Results may differ from a plain program's by a relative error of at most 0.0085.
Values may be sent and summed in bfloat16 or wider, within the bound.
A program may use at most 64 MiB of HBM per device.

v0:
```python
import math

import jax
import jax.numpy as jnp
from jax import lax
from jax.sharding import PartitionSpec as P


def from_everyone(value, axis):
    copies = jnp.broadcast_to(value, (lax.axis_size(axis), *value.shape))
    return lax.all_to_all(copies, axis, split_axis=0, concat_axis=0, tiled=True)


def of_everyone(value, axis):
    everything = from_everyone(value, axis)
    return jnp.sum(everything, axis=0)


def in_one(arrays, axis):
    ends = [0]
    for a in arrays:
        ends.append(ends[-1] + a.size)
    total = of_everyone(jnp.concatenate([a.ravel() for a in arrays]), axis)
    return tuple((total[b:e].reshape(a.shape) for a, b, e in zip(arrays, ends, ends[1:])))


def phase_tables(waves, width):
    points = jnp.arange(width, dtype=jnp.int32)
    phase = (waves[:, None] * points[None, :] % width).astype(jnp.float32) * (2.0 * math.pi / width)
    return (jnp.cos(phase), jnp.sin(phase))


def block_weight(mixing):
    real_part = mixing[:, 0]
    imag_part = mixing[:, 1]
    upper = jnp.concatenate([real_part, imag_part], axis=2)
    lower = jnp.concatenate([-imag_part, real_part], axis=2)
    return jnp.concatenate([upper, lower], axis=1)


def per_device(field, gain, slot_wave, legendre, mixing):
    lat_count = lax.axis_size("lat")
    lat_dev, width, chans = field.shape
    slot_dev, degs, nlat = legendre.shape
    count = float(lat_dev * lat_count * width)
    values = field.astype(jnp.float32)
    local_sum = jnp.sum(values, axis=(0, 1))
    local_sq = jnp.sum(values * values, axis=(0, 1))
    total, squares = in_one((local_sum, local_sq), "lat")
    mean = total / count
    var = squares / count - mean * mean
    normed = ((values - mean) * (gain / jnp.sqrt(var + 1e-05))).astype(jnp.bfloat16)
    cosine, sine = phase_tables(slot_wave, width)
    forward = jnp.stack([cosine, -sine]).astype(jnp.bfloat16).reshape(2, lat_count, slot_dev, width)
    weight_m = jnp.where(slot_wave == 0, 1.0, 2.0).astype(jnp.float32)[:, None]
    inverse = jnp.stack([weight_m * cosine, -weight_m * sine]).astype(jnp.bfloat16)
    inv_root = 1.0 / math.sqrt(width)
    spectrum = (
        jnp.einsum("anc,rdjn->dajrc", normed, forward, preferred_element_type=jnp.float32)
        * inv_root
    )
    spectrum = spectrum.astype(jnp.bfloat16).reshape(lat_count, lat_dev, slot_dev, 2 * chans)
    arrived = lax.all_to_all(spectrum, "lat", split_axis=0, concat_axis=1, tiled=True)[0]
    mine = lax.dynamic_slice_in_dim(slot_wave, lax.axis_index("lat") * slot_dev, slot_dev, 0)
    big = block_weight(mixing)
    lat_scale = math.sqrt(nlat / degs)
    degrees = jnp.arange(degs, dtype=jnp.int32)
    coef = jnp.einsum("jlt,tjc->jlc", legendre, arrived, preferred_element_type=jnp.float32)
    coef = jnp.where((degrees[None, :] >= mine[:, None])[:, :, None], coef, 0.0).astype(
        jnp.bfloat16
    )
    mixed = jnp.einsum("jlc,jcd->jld", coef, big, preferred_element_type=jnp.float32).astype(
        jnp.bfloat16
    )
    back = (
        jnp.einsum("jlt,jld->tjd", legendre, mixed, preferred_element_type=jnp.float32) * lat_scale
    )
    back = back.astype(jnp.bfloat16)
    back = back.reshape(lat_count, lat_dev, slot_dev, 2 * chans)
    returned = lax.all_to_all(back, "lat", split_axis=0, concat_axis=2, tiled=True)[0]
    returned = returned.reshape(lat_dev, slot_dev * lat_count, 2, chans)
    filtered = (
        jnp.einsum("akrc,rkn->anc", returned, inverse, preferred_element_type=jnp.float32)
        * inv_root
    )
    return (normed.astype(jnp.float32) + filtered).astype(jnp.bfloat16)


def solution(mesh):
    return jax.shard_map(
        per_device,
        mesh=mesh,
        in_specs=(
            P(("member", "lat"), None, None),
            P(),
            P(),
            P("lat", None, None),
            P("lat", None, None, None),
        ),
        out_specs=P(("member", "lat"), None, None),
        check_vma=False,
    )
```

profile of v0, /device:TPU:37, one launch (start us, length us, event | category | flops | bytes accessed | tf_op | source)
XLA Modules:
  0.0 713.9 jit_solution(15782065350737773823)
XLA Ops:
  0.0 0.0 copy-start
  0.0 3.6 convert_reduce_fusion
  3.6 0.0 copy-start.3
  3.6 0.7 broadcast_in_dim.31
  4.3 34.3 %all-to-all-start = ((f32[64,1,512]{2,1,0:T(1,128)}), f32[64,1,512]{2,1,0:T(1,128)S(1)}, u32[]{:S(2)}, u32[]{:S(2)}) async-start(f32[64,1,512]{2,1,0:T(1,128)} %broadcast_in_dim.31), calls=%async_computation | async-start | bytes 262144 | tf_op jit(solution)/shard_map/all_to_all | solution.py:11
  38.7 0.0 copy-done.2
  38.7 0.1 mul.154
  38.8 0.1 copy.49
  38.9 11.6 %cosine_convert_fusion = (bf16[1,64,6,1440]{3,1,2,0:T(8,128)(2,1)S(1)}, bf16[1,64,6,1440]{3,1,2,0:T(8,128)(2,1)}) fusion(s32[64,6]{0,1:T(8,128)S(1)} %copy.49), kind=kLoop, calls=%fused_computation.37 | loop fusion | flops 6635520 | bytes 2213376 | tf_op jit(solution)/shard_map/convert
  50.5 18.2 %all-to-all-done = f32[64,1,512]{2,1,0:T(1,128)S(1)} async-done(((f32[64,1,512]{2,1,0:T(1,128)}), f32[64,1,512]{2,1,0:T(1,128)S(1)}, u32[]{:S(2)}, u32[]{:S(2)}) %all-to-all-start) | async-done | bytes 131104 | tf_op jit(solution)/shard_map/all_to_all | solution.py:11
  68.7 0.1 reduce_sum.29
  68.8 0.0 copy-done.3
  68.8 6.5 fusion.17
  75.3 3.8 copy.67
  79.1 6.8 reshape.227
  85.9 7.6 %all-to-all-start.1 = ((bf16[64,6,6,512]{3,2,1,0:T(8,128)(2,1)}), bf16[64,6,6,512]{3,2,1,0:T(8,128)(2,1)}, u32[]{:S(2)}, u32[]{:S(2)}) async-start(bf16[64,6,6,512]{3,2,1,0:T(8,128)(2,1)} %reshape.227), calls=%async_computation.1 | async-start | bytes 6291456 | tf_op jit(solution)/shard_map/all_to_all | solution.py:63
  93.6 0.1 dynamic_slice.3
  93.7 0.1 iota_compare_fusion
  93.7 0.0 copy-done.1
  93.7 1.0 fusion.50
  94.7 1.3 slice_bitcast_fusion
  96.0 287.9 %all-to-all-done.1 = bf16[64,6,6,512]{3,2,1,0:T(8,128)(2,1)} async-done(((bf16[64,6,6,512]{3,2,1,0:T(8,128)(2,1)}), bf16[64,6,6,512]{3,2,1,0:T(8,128)(2,1)}, u32[]{:S(2)}, u32[]{:S(2)}) %all-to-all-start.1) | async-done | bytes 2359328 | tf_op jit(solution)/shard_map/all_to_all | solution.py:63
  383.9 0.0 copy-done
  383.9 8.1 %fusion.7 = bf16[6,384,512]{2,1,0:T(8,128)(2,1)} fusion(bf16[6,256,256]{2,1,0:T(8,128)(2,1)} %get-tuple-element.8, bf16[6,256,256]{2,1,0:T(8,128)(2,1)} %fusion.50, bf16[6,256,256]{2,1,0:T(8,128)(2,1)} %get-tuple-element.7, pred[6,384]{1,0:T(8,128)(4,1)S(1)} %iota_compare_fusion, bf16[6,384,384]{2,1,0:T(8,128)(2,1)S(1)} %copy-done, ...), kind=kOutput, calls=%fused_computation.15 | convolution fusion | flops 2128871424 | bytes 8849664 | tf_op jit(solution)/shard_map/jlc,jcd->jld/dot_general | solution.py:72
  392.0 4.5 convert_bitcast_fusion
  396.5 5.0 reshape.222
  401.5 4.0 copy.58
  405.5 6.2 all-to-all-start.2
  411.8 10.5 %multiply_convert_fusion.2 = (bf16[1,384,1440]{1,2,0:T(8,128)(2,1)S(1)}, bf16[1,384,1440]{1,2,0:T(8,128)(2,1)}) fusion(s32[384]{0:T(512)S(1)} %copy-done.2, f32[384]{0:T(512)S(1)} %get-tuple-element.13, f32[384]{0:T(512)S(1)} %get-tuple-element.14), kind=kLoop, calls=%fused_computation.49 | loop fusion | flops 7188480 | bytes 2216448 | tf_op jit(solution)/shard_map/convert.2
  422.2 275.7 %all-to-all-done.2 = bf16[64,6,6,512]{3,1,2,0:T(8,128)(2,1)} async-done(((bf16[64,6,6,512]{3,1,2,0:T(8,128)(2,1)}), bf16[64,6,6,512]{3,1,2,0:T(8,128)(2,1)}, u32[]{:S(2)}, u32[]{:S(2)}) %all-to-all-start.2) | async-done | bytes 2359328 | tf_op jit(solution)/shard_map/all_to_all | solution.py:80
  697.9 6.5 reshape.228
  704.5 9.4 %fusion.3 = bf16[6,1440,256]{2,1,0:T(8,128)(2,1)} fusion(f32[256]{0:T(256)S(1)} %get-tuple-element.16, f32[256]{0:T(256)S(1)} %get-tuple-element.15, bf16[6,1440,256]{2,1,0:T(8,128)(2,1)} %param.5, bf16[6,384,2,256]{3,2,0,1:T(2,128)(2,1)} %reshape.228, bf16[1,384,1440]{1,2,0:T(8,128)(2,1)} %get-tuple-element.12, bf16[1,384,1440]{1,2,0:T(8,128)(2,1)S(1)} %get-tuple-element.11), kind=kOutput, calls=%fused_computation.7 | convolution fusion | flops 3419504640 | bytes 13420544 | tf_op jit(solution)/shard_map/akrc,rkn->anc/dot_general | solution.py:83
  (5 shorter events, 0.0 us)
Async XLA Ops:
  0.0 383.9 %copy-start = (bf16[6,384,384]{2,1,0:T(8,128)(2,1)S(1)}, bf16[6,384,384]{2,1,0:T(8,128)(2,1)}, u32[]{:S(2)}) copy-start(bf16[6,384,384]{2,1,0:T(8,128)(2,1)} %param.8) | copy-start | bytes 5308420
  0.0 38.7 %copy-start.2 = (s32[384]{0:T(512)S(1)}, s32[384]{0:T(512)}, u32[]{:S(2)}) copy-start(s32[384]{0:T(512)} %param.7) | copy-start | bytes 4612
  3.6 65.2 %copy-start.3 = (f32[256]{0:T(256)S(1)}, f32[256]{0:T(256)}, u32[]{:S(2)}) copy-start(f32[256]{0:T(256)} %param.6) | copy-start | bytes 3076
  4.3 64.4 %all-to-all-start = ((f32[64,1,512]{2,1,0:T(1,128)}), f32[64,1,512]{2,1,0:T(1,128)S(1)}, u32[]{:S(2)}, u32[]{:S(2)}) async-start(f32[64,1,512]{2,1,0:T(1,128)} %broadcast_in_dim.31), calls=%async_computation | async-start | bytes 262144 | tf_op jit(solution)/shard_map/all_to_all | solution.py:11
  85.9 7.8 %copy-start.1 = (bf16[6,2,256,256]{3,2,1,0:T(8,128)(2,1)S(1)}, bf16[6,2,256,256]{3,2,1,0:T(8,128)(2,1)}, u32[]{:S(2)}) copy-start(bf16[6,2,256,256]{3,2,1,0:T(8,128)(2,1)} %param.9) | copy-start | bytes 4718596
  85.9 297.9 %all-to-all-start.1 = ((bf16[64,6,6,512]{3,2,1,0:T(8,128)(2,1)}), bf16[64,6,6,512]{3,2,1,0:T(8,128)(2,1)}, u32[]{:S(2)}, u32[]{:S(2)}) async-start(bf16[64,6,6,512]{3,2,1,0:T(8,128)(2,1)} %reshape.227), calls=%async_computation.1 | async-start | bytes 6291456 | tf_op jit(solution)/shard_map/all_to_all | solution.py:63
  405.5 292.4 %all-to-all-start.2 = ((bf16[64,6,6,512]{3,1,2,0:T(8,128)(2,1)}), bf16[64,6,6,512]{3,1,2,0:T(8,128)(2,1)}, u32[]{:S(2)}, u32[]{:S(2)}) async-start(bf16[64,6,6,512]{3,1,2,0:T(8,128)(2,1)} %copy.58), calls=%async_computation.2 | async-start | bytes 6291456 | tf_op jit(solution)/shard_map/all_to_all | solution.py:80
where the time goes:
time: 718 us; the launch traced here: 714 us
  waiting for transfers between devices  582 us (81%)
  starting transfers between devices  48.2 us (7%)
  local copies, waits for them, and re-layouts  28.5 us (4%)
  matrix products  28.5 us (4%)
  other arithmetic  26.8 us (4%)
    all_to_all x1, waiting for transfers between devices, per_device(): lax.all_to_all(spectrum, 'lat', split_axis=0, concat_axis=1, tiled=True)[0]  288 us
    all_to_all x1, waiting for transfers between devices, per_device(): lax.all_to_all(back, 'lat', split_axis=0, concat_axis=2, tiled=True)[0]  276 us
    all_to_all x1, starting transfers between devices, from_everyone(): return lax.all_to_all(copies, axis, split_axis=0, concat_axis=0, tiled=True)  34.3 us
    another operation x2, other arithmetic  22.1 us
    all_to_all x1, waiting for transfers between devices, from_everyone(): return lax.all_to_all(copies, axis, split_axis=0, concat_axis=0, tiled=True)  18.2 us
  transfers between devices with their start and end apart: 3, of which 3 were waited for; matrix products, arithmetic and copies ran while one was open for 3% of the time, Pallas kernels for 0%

commit v1 on v0

v1 whole, which is shorter than its diff:
```python
import functools
import math

import jax
import jax.numpy as jnp
from jax import lax
from jax.experimental import pallas as pl
from jax.experimental.pallas import tpu as pltpu
from jax.sharding import PartitionSpec as P

MESH = pl.DeviceIdType.MESH


def exchange_kernel(count, each, x_ref, o_ref, send_sem, recv_sem, local_sem):
    me = lax.axis_index("lat")
    barrier = pltpu.get_barrier_semaphore()

    def greet(k, carry):
        pl.semaphore_signal(
            barrier, inc=1, device_id={"lat": lax.rem(me + k, count)}, device_id_type=MESH
        )
        return carry

    lax.fori_loop(1, count, greet, 0)
    pl.semaphore_wait(barrier, count - 1)
    own = pltpu.make_async_copy(x_ref.at[me] if each else x_ref, o_ref.at[me], local_sem)
    own.start()

    def send(k, carry):
        for step in (k, count - k):
            there = lax.rem(me + step, count)
            pltpu.make_async_remote_copy(
                src_ref=x_ref.at[there] if each else x_ref,
                dst_ref=o_ref.at[me],
                send_sem=send_sem,
                recv_sem=recv_sem,
                device_id={"lat": there},
                device_id_type=MESH,
            ).start()
        return carry

    lax.fori_loop(1, count // 2, send, 0)
    there = lax.rem(me + count // 2, count)
    pltpu.make_async_remote_copy(
        src_ref=x_ref.at[there] if each else x_ref,
        dst_ref=o_ref.at[me],
        send_sem=send_sem,
        recv_sem=recv_sem,
        device_id={"lat": there},
        device_id_type=MESH,
    ).start()
    own.wait()
    others = o_ref.at[pl.ds(0, count - 1)]
    pltpu.make_async_copy(others, others, send_sem).wait()
    pltpu.make_async_copy(others, others, recv_sem).wait()


def exchange(x, each, name, ident):
    count = lax.axis_size("lat")
    block = x.shape[1:] if each else x.shape
    return pl.pallas_call(
        functools.partial(exchange_kernel, count, each),
        out_shape=jax.ShapeDtypeStruct((count, *block), x.dtype),
        in_specs=[pl.BlockSpec(memory_space=pltpu.VMEM)],
        out_specs=pl.BlockSpec(memory_space=pltpu.VMEM),
        scratch_shapes=[pltpu.SemaphoreType.DMA] * 3,
        compiler_params=pltpu.CompilerParams(collective_id=ident, has_side_effects=True),
        name=name,
    )(x)


def phase_tables(waves, width):
    points = jnp.arange(width, dtype=jnp.int32)
    phase = (waves[:, None] * points[None, :] % width).astype(jnp.float32) * (2.0 * math.pi / width)
    return (jnp.cos(phase), jnp.sin(phase))


def block_weight(mixing):
    real_part = mixing[:, 0]
    imag_part = mixing[:, 1]
    upper = jnp.concatenate([real_part, imag_part], axis=2)
    lower = jnp.concatenate([-imag_part, real_part], axis=2)
    return jnp.concatenate([upper, lower], axis=1)


def per_device(field, gain, slot_wave, legendre, mixing):
    lat_count = lax.axis_size("lat")
    lat_dev, width, chans = field.shape
    slot_dev, degs, nlat = legendre.shape
    count = float(lat_dev * lat_count * width)
    values = field.astype(jnp.float32)
    local = jnp.stack([jnp.sum(values, axis=(0, 1)), jnp.sum(values * values, axis=(0, 1))])
    total, squares = jnp.sum(exchange(local, False, "sums", 0), axis=0)
    mean = total / count
    var = squares / count - mean * mean
    normed = ((values - mean) * (gain / jnp.sqrt(var + 1e-05))).astype(jnp.bfloat16)
    cosine, sine = phase_tables(slot_wave, width)
    table = jnp.stack([cosine, -sine], axis=1).astype(jnp.bfloat16)
    weight_m = jnp.where(slot_wave == 0, 1.0, 2.0).astype(jnp.bfloat16)[:, None, None]
    inv_root = 1.0 / math.sqrt(width)
    spectrum = (
        jnp.einsum("krn,anc->krac", table, normed, preferred_element_type=jnp.float32) * inv_root
    )
    spectrum = spectrum.astype(jnp.bfloat16).reshape(lat_count, -1, chans)
    arrived = exchange(spectrum, True, "there", 1)
    arrived = arrived.reshape(lat_count, slot_dev, 2, lat_dev, chans)
    arrived = arrived.transpose(1, 0, 3, 2, 4).reshape(slot_dev, nlat, 2 * chans)
    mine = lax.dynamic_slice_in_dim(slot_wave, lax.axis_index("lat") * slot_dev, slot_dev, 0)
    big = block_weight(mixing)
    lat_scale = math.sqrt(nlat / degs)
    degrees = jnp.arange(degs, dtype=jnp.int32)
    coef = jnp.einsum("jlt,jtc->jlc", legendre, arrived, preferred_element_type=jnp.float32)
    coef = jnp.where((degrees[None, :] >= mine[:, None])[:, :, None], coef, 0.0).astype(
        jnp.bfloat16
    )
    mixed = jnp.einsum("jlc,jcd->jld", coef, big, preferred_element_type=jnp.float32).astype(
        jnp.bfloat16
    )
    back = (
        jnp.einsum("jlt,jld->jtd", legendre, mixed, preferred_element_type=jnp.float32) * lat_scale
    )
    back = back.astype(jnp.bfloat16).reshape(slot_dev, lat_count, lat_dev, 2, chans)
    back = back.transpose(1, 0, 3, 2, 4).reshape(lat_count, -1, chans)
    returned = exchange(back, True, "home", 2)
    returned = returned.reshape(slot_dev * lat_count, 2, lat_dev, chans)
    filtered = (
        jnp.einsum(
            "krac,krn->anc", returned * weight_m[..., None], table, preferred_element_type=jnp.float32
        )
        * inv_root
    )
    return (normed.astype(jnp.float32) + filtered).astype(jnp.bfloat16)


def solution(mesh):
    return jax.shard_map(
        per_device,
        mesh=mesh,
        in_specs=(
            P(("member", "lat"), None, None),
            P(),
            P(),
            P("lat", None, None),
            P("lat", None, None, None),
        ),
        out_specs=P(("member", "lat"), None, None),
        check_vma=False,
    )
```

time: 718 us -> 599 us (0.83)
  waiting for transfers between devices: 582 us -> 0 us
  Pallas kernels: 0 us -> 509 us
  starting transfers between devices: 48.2 us -> 0 us
  local copies, waits for them, and re-layouts: 28.5 us -> 42.6 us
  other arithmetic: 26.8 us -> 18.6 us
    all_to_all x3 -> x0, waiting for transfers between devices: 582 us -> none  [the longest x1 288 us: per_device(): lax.all_to_all(spectrum, 'lat', split_axis=0, concat_axis=1, tiled=True)[0]]
    pallas_call x0 -> x3, Pallas kernels: none -> 509 us  [exchange(): pl.pallas_call(functools.partial(exchange_kernel, count, each), out_shape...]
    all_to_all x3 -> x0, starting transfers between devices: 48.2 us -> none  [the longest x1 34.3 us: from_everyone(): return lax.all_to_all(copies, axis, split_axis=0, concat_axis=0, tiled=True)]
    another operation x2, other arithmetic: 22.1 us -> 10.1 us
    convert_element_type x0 -> x2, local copies, waits for them, and re-layouts: none -> 7.37 us  [the longest x1 4.27 us: per_device(): back.astype(jnp.bfloat16).reshape(slot_dev, lat_count, lat_dev, 2, chans)]
    reshape x4 -> x5, local copies, waits for them, and re-layouts: 19.7 us -> 25.7 us  [the longest x1 6.55 us: per_device(): arrived.transpose(1, 0, 3, 2, 4).reshape(slot_dev, nlat, 2 * chans)]
  transfers between devices with their start and end apart: 3 -> 0, of which waited for: 3 -> 0; matrix products, arithmetic and copies ran while one was open for 3% -> 0% of each run, Pallas kernels for 0% -> 0%
where the time goes in v1:
time: 599 us; the launch traced here: 598 us
  Pallas kernels  509 us (85%)
  local copies, waits for them, and re-layouts  42.6 us (7%)
  matrix products  27.1 us (5%)
  other arithmetic  18.6 us (3%)
    pallas_call x3, Pallas kernels, exchange(): pl.pallas_call(functools.partial(exchange_kernel, count, each), out_shape...  509 us

profile of v1, /device:TPU:37, one launch (start us, length us, event | category | flops | bytes accessed | tf_op | source)
XLA Modules:
  0.0 597.8 jit_solution(11441610898696217332)
XLA Ops:
  0.0 0.0 copy-start
  0.0 3.6 convert_reduce_fusion
  3.6 0.6 pad_maximum_fusion.3.x_ref
  4.2 53.0 %sums.1 = f32[64,2,256]{2,1,0:T(2,128)} custom-call(f32[2,256]{1,0:T(2,128)} %pad_maximum_fusion.3.x_ref), custom_call_target="tpu_custom_call" | custom-call | tf_op jit(solution)/shard_map/sums/pallas_call | solution.py:61
  57.2 1.0 reduce_sum.29
  58.2 0.0 copy-done.7
  58.2 0.0 copy-done.6
  58.2 9.5 %cosine_convert_fusion = (bf16[384,1,1440]{0,2,1:T(8,128)(2,1)S(1)}, bf16[384,1,1440]{0,2,1:T(8,128)(2,1)S(1)}) fusion(s32[384]{0:T(512)S(1)} %copy-done.6), kind=kLoop, calls=%fused_computation.34 | loop fusion | flops 6635520 | bytes 2213376 | tf_op jit(solution)/shard_map/convert
  67.8 0.0 copy-start.2
  67.8 0.0 copy-start.4
  67.8 7.4 %multiply_convert_fusion = bf16[384,2,6,256]{3,0,2,1:T(8,128)(2,1)S(1)} fusion(f32[256]{0:T(256)S(1)} %rsqrt_multiply_fusion, f32[256]{0:T(256)S(1)} %bitcast.50, bf16[6,1440,256]{2,1,0:T(8,128)(2,1)} %param.5, bf16[384,1,1440]{0,2,1:T(8,128)(2,1)S(1)} %get-tuple-element.10, bf16[384,1,1440]{0,2,1:T(8,128)(2,1)S(1)} %get-tuple-element.9), kind=kOutput, calls=%fused_computation.10 | convolution fusion | flops 3413016576 | bytes 8996864 | tf_op jit(solution)/shard_map/krn,anc->krac/dot_general | solution.py:102
  75.2 0.0 copy-done.2
  75.2 3.1 copy.10
  78.3 5.2 reshape.129.x_ref
  83.5 229.0 %there.1 = bf16[64,72,256]{2,1,0:T(8,128)(2,1)} custom-call(bf16[64,72,256]{2,1,0:T(8,128)(2,1)} %reshape.129.x_ref), custom_call_target="tpu_custom_call" | custom-call | tf_op jit(solution)/shard_map/there/pallas_call | solution.py:61
  312.5 2.2 copy.11
  314.8 3.8 copy.12
  318.6 6.6 %reshape.131 = bf16[6,384,512]{2,1,0:T(8,128)(2,1)} reshape(bf16[6,64,6,2,256]{4,3,2,1,0:T(2,128)(2,1)} %copy.12) | data formatting | bytes 4718592 | tf_op jit(solution)/shard_map/reshape | solution.py:107
  325.1 0.1 dynamic_slice.3
  325.2 0.1 iota_compare_fusion
  325.3 1.2 slice_bitcast_fusion
  326.5 0.9 fusion.39
  327.5 7.4 %fusion.7 = bf16[6,384,512]{1,2,0:T(8,128)(2,1)} fusion(bf16[6,256,256]{2,1,0:T(8,128)(2,1)} %get-tuple-element.8, bf16[6,256,256]{2,1,0:T(8,128)(2,1)} %fusion.39, bf16[6,256,256]{2,1,0:T(8,128)(2,1)} %get-tuple-element.7, pred[6,384]{1,0:T(8,128)(4,1)S(1)} %iota_compare_fusion, bf16[6,384,512]{2,1,0:T(8,128)(2,1)} %reshape.131, ...), kind=kOutput, calls=%fused_computation.14 | convolution fusion | flops 2128871424 | bytes 8849664 | tf_op jit(solution)/shard_map/jlc,jcd->jld/dot_general | solution.py:116
  334.9 4.7 convert_bitcast_fusion
  339.5 4.3 copy.14
  343.8 6.1 %reshape.132 = bf16[6,64,6,2,256]{4,3,2,1,0:T(2,128)(2,1)} reshape(bf16[6,384,512]{2,1,0:T(8,128)(2,1)} %copy.14) | data formatting | bytes 4718592 | tf_op jit(solution)/shard_map/reshape | solution.py:122
  349.9 2.1 copy.15
  352.0 2.7 copy.16.x_ref
  354.7 227.2 %home.1 = bf16[64,72,256]{2,1,0:T(8,128)(2,1)} custom-call(bf16[64,72,256]{2,1,0:T(8,128)(2,1)} %copy.16.x_ref), custom_call_target="tpu_custom_call" | custom-call | tf_op jit(solution)/shard_map/home/pallas_call | solution.py:61
  582.0 5.1 reshape.134
  587.1 2.9 broadcast_multiply_fusion
  590.1 7.7 %fusion.3 = bf16[6,1440,256]{2,1,0:T(8,128)(2,1)} fusion(f32[256]{0:T(256)S(1)} %rsqrt_multiply_fusion, f32[256]{0:T(256)S(1)} %bitcast.51, bf16[6,1440,256]{2,1,0:T(8,128)(2,1)} %param.5, bf16[384,2,6,256]{3,2,1,0:T(8,128)(2,1)S(1)} %broadcast_multiply_fusion, bf16[384,1,1440]{0,2,1:T(8,128)(2,1)S(1)} %copy-done.5, bf16[384,1,1440]{0,2,1:T(8,128)(2,1)S(1)} %copy-done.3), kind=kOutput, calls=%fused_computation.7 | convolution fusion | flops 3419504640 | bytes 13420544 | tf_op jit(solution)/shard_map/krac,krn->anc/dot_general | solution.py:127
  (13 shorter events, 0.0 us)
Async XLA Ops:
  0.0 327.5 %copy-start = (bf16[6,384,384]{2,1,0:T(8,128)(2,1)S(1)}, bf16[6,384,384]{2,1,0:T(8,128)(2,1)}, u32[]{:S(2)}) copy-start(bf16[6,384,384]{2,1,0:T(8,128)(2,1)} %param.8) | copy-start | bytes 5308420
  0.0 58.2 %copy-start.7 = (f32[256]{0:T(256)S(1)}, f32[256]{0:T(256)}, u32[]{:S(2)}) copy-start(f32[256]{0:T(256)} %param.6) | copy-start | bytes 3076
  0.0 58.2 %copy-start.6 = (s32[384]{0:T(512)S(1)}, s32[384]{0:T(512)}, u32[]{:S(2)}) copy-start(s32[384]{0:T(512)} %param.7) | copy-start | bytes 4612
  67.8 7.4 %copy-start.2 = (bf16[384,1,1440]{0,2,1:T(8,128)(2,1)}, bf16[384,1,1440]{0,2,1:T(8,128)(2,1)S(1)}, u32[]{:S(2)}) copy-start(bf16[384,1,1440]{0,2,1:T(8,128)(2,1)S(1)} %get-tuple-element.9) | copy-start | bytes 3317764
  67.8 7.4 %copy-start.4 = (bf16[384,1,1440]{0,2,1:T(8,128)(2,1)}, bf16[384,1,1440]{0,2,1:T(8,128)(2,1)S(1)}, u32[]{:S(2)}) copy-start(bf16[384,1,1440]{0,2,1:T(8,128)(2,1)S(1)} %get-tuple-element.10) | copy-start | bytes 3317764
  318.6 6.7 %copy-start.1 = (bf16[6,2,256,256]{3,2,1,0:T(8,128)(2,1)S(1)}, bf16[6,2,256,256]{3,2,1,0:T(8,128)(2,1)}, u32[]{:S(2)}) copy-start(bf16[6,2,256,256]{3,2,1,0:T(8,128)(2,1)} %param.9) | copy-start | bytes 4718596
  587.1 2.9 copy-start.3
  587.1 3.0 copy-start.5

commit v2 on v0

v2 whole, which is shorter than its diff:
```python
import functools
import math

import jax
import jax.numpy as jnp
import numpy as np
from jax import lax
from jax.experimental import pallas as pl
from jax.experimental.pallas import tpu as pltpu
from jax.sharding import PartitionSpec as P

MESH = pl.DeviceIdType.MESH
F32 = jnp.float32
BF16 = jnp.bfloat16
HALVES = 2
PER_CHUNK = 2
GROUP = HALVES * PER_CHUNK * 2


def dot(a, b):
    return jnp.dot(a, b, preferred_element_type=F32)


def dot_tn(a, b):
    return lax.dot_general(a, b, (((0,), (0,)), ((), ())), preferred_element_type=F32)


def dot_nt(a, b):
    return lax.dot_general(a, b, (((1,), (1,)), ((), ())), preferred_element_type=F32)


def one_hot(target, rows):
    wide = jnp.broadcast_to(target, (rows, target.shape[1]))
    at = lax.broadcasted_iota(jnp.int32, wide.shape, 0)
    return jnp.where(at == wide, 1.0, 0.0).astype(BF16)


def layer_kernel(
    count,
    total_count,
    wave_ref,
    rowsum_ref,
    index_ref,
    lat_old_ref,
    lat_new_ref,
    gather_ref,
    scatter_ref,
    gain_ref,
    field_hbm,
    cos_hbm,
    legendre_hbm,
    mixing_hbm,
    out_hbm,
    field_v,
    cos_v,
    legendre_v,
    mixing_v,
    table_v,
    table_t_v,
    out_one,
    in_one,
    out_two,
    in_two,
    leg_v,
    leg_t_v,
    big_v,
    spec_v,
    z_v,
    masked_v,
    acc_v,
    mine_v,
    stats_v,
    shift_v,
    scale_v,
    send_sem,
    stat_sem,
    recv_one,
    recv_two,
    load_sem,
    store_sem,
):
    me = lax.axis_index("lat")
    lat_dev, width, chans = field_v.shape
    slots, degs, nlat = legendre_v.shape
    thirds = lat_dev // HALVES
    chunks = slots // PER_CHUNK
    rows = count * GROUP
    fold = HALVES * count
    inv_root = 1.0 / math.sqrt(width)
    lat_scale = math.sqrt(nlat / degs)

    barrier = pltpu.get_barrier_semaphore()

    def greet(k, carry):
        pl.semaphore_signal(
            barrier, inc=1, device_id={"lat": lax.rem(me + k, count)}, device_id_type=MESH
        )
        return carry

    lax.fori_loop(1, count, greet, 0)

    loads = [
        pltpu.make_async_copy(src, dst, load_sem.at[i])
        for i, (src, dst) in enumerate(
            (
                (field_hbm, field_v),
                (cos_hbm, cos_v),
                (legendre_hbm, legendre_v),
                (mixing_hbm, mixing_v),
            )
        )
    ]
    for load in loads:
        load.start()
    loads[0].wait()

    part = width // 10
    local_count = float(lat_dev * width)

    def add_rows(i, total):
        block = field_v[i // 10, pl.ds(pl.multiple_of((i % 10) * part, 16), part), :]
        return total + jnp.sum(block.astype(F32), axis=0, keepdims=True)

    mean_here = lax.fori_loop(0, lat_dev * 10, add_rows, jnp.zeros((1, chans), F32)) / local_count

    def add_squares(i, total):
        block = field_v[i // 10, pl.ds(pl.multiple_of((i % 10) * part, 16), part), :]
        off = block.astype(F32) - mean_here
        return total + jnp.sum(off * off, axis=0, keepdims=True)

    squares_here = lax.fori_loop(0, lat_dev * 10, add_squares, jnp.zeros((1, chans), F32))
    mine_v[0:1, :] = mean_here
    mine_v[1:2, :] = squares_here
    stats_v[me] = mine_v[...]

    loads[1].wait()

    def build_table(k, carry):
        table_v[k] = dot_tn(one_hot(index_ref[k], cos_v.shape[0]), cos_v[...]).astype(BF16)
        return carry

    row_half = lax.broadcasted_iota(jnp.int32, (rows, chans), 0) // (GROUP // HALVES) % HALVES

    def transform(k):
        sums = dot(table_v[k], jnp.ones((width, 128), BF16))[:, :1]

        def third(t, carry):
            low = dot(table_v[k], field_v[t])
            high = dot(table_v[k], field_v[thirds + t])
            both = (jnp.where(row_half == 0, low, high) - sums * mean_here) * inv_root
            out_one[
                pl.ds(k * count, count), :, pl.ds(pl.multiple_of(t * chans, 128), chans)
            ] = both.reshape(count, GROUP, chans).astype(BF16)
            return carry

        lax.fori_loop(0, thirds, third, 0)
        in_one[k * count + me] = out_one[k * count + me]

    def send_chunk(k, src, dst, recv):
        def send(there):
            pltpu.make_async_remote_copy(
                src_ref=src.at[k * count + there],
                dst_ref=dst.at[k * count + me],
                send_sem=send_sem,
                recv_sem=recv.at[k],
                device_id={"lat": there},
                device_id_type=MESH,
            ).start()

        def both(i, carry):
            send(lax.rem(me + i, count))
            send(lax.rem(me + count - i, count))
            return carry

        lax.fori_loop(1, count // 2, both, 0)
        send(lax.rem(me + count // 2, count))

    def wait_chunk(k, dst, recv):
        others = dst.at[pl.ds(k * count, count - 1)]
        pltpu.make_async_copy(others, others, recv.at[k]).wait()

    build_table(0, 0)
    transform(0)
    pl.semaphore_wait(barrier, count - 1)

    def send_stats(i, carry):
        there = lax.rem(me + i, count)
        pltpu.make_async_remote_copy(
            src_ref=mine_v,
            dst_ref=stats_v.at[me],
            send_sem=stat_sem.at[0],
            recv_sem=stat_sem.at[1],
            device_id={"lat": there},
            device_id_type=MESH,
        ).start()
        return carry

    lax.fori_loop(1, count, send_stats, 0)
    send_chunk(0, out_one, in_one, recv_one)

    def rest(k, carry):
        build_table(k, 0)
        transform(k)
        send_chunk(k, out_one, in_one, recv_one)
        return carry

    lax.fori_loop(1, chunks, rest, 0)

    loads[2].wait()
    loads[3].wait()

    def prepare(s, carry):
        leg_v[s] = dot(legendre_v[s], one_hot(lat_old_ref[...], nlat)).astype(BF16)
        leg_t_v[s] = dot_nt(one_hot(lat_new_ref[...], nlat), legendre_v[s]).astype(BF16)
        real = mixing_v[s, 0]
        imag = mixing_v[s, 1]
        big_v[s, :chans, :chans] = real
        big_v[s, :chans, chans:] = imag
        big_v[s, chans:, :chans] = -imag
        big_v[s, chans:, chans:] = real
        return carry

    lax.fori_loop(0, slots, prepare, 0)

    waves = cos_v.shape[0] // 2
    table_row = lax.broadcasted_iota(jnp.int32, (2 * waves, rows), 0)
    weight = jnp.where((table_row == 0) | (table_row == waves), 1.0, 2.0)

    def build_table_t(k, carry):
        chosen = (one_hot(index_ref[k], 2 * waves).astype(F32) * weight).astype(BF16)
        table_t_v[k] = dot_tn(cos_v[...], chosen).astype(BF16)
        return carry

    lax.fori_loop(0, chunks, build_table_t, 0)

    pltpu.make_async_copy(
        stats_v.at[pl.ds(0, count - 1)], stats_v.at[pl.ds(0, count - 1)], stat_sem.at[1]
    ).wait()
    means = stats_v[:, 0, :]
    mean = jnp.sum(means, axis=0, keepdims=True) / float(count)
    apart = means - mean
    var = (
        jnp.sum(stats_v[:, 1, :], axis=0, keepdims=True)
        + local_count * jnp.sum(apart * apart, axis=0, keepdims=True)
    ) / total_count
    scale = gain_ref[...] / jnp.sqrt(var + 1e-05)
    scale_v[0:1, :] = mean
    scale_v[1:2, :] = scale
    for h in range(HALVES):
        shift_v[h * count : (h + 1) * count, :] = apart * scale * inv_root

    def middle(k, carry):
        wait_chunk(k, in_one, recv_one)
        arrived = in_one[pl.ds(k * count, count)].reshape(rows, thirds * chans)
        ordered = dot(one_hot(gather_ref[...], rows), arrived)
        for q in range(PER_CHUNK * 2):
            j, r = q // 2, q % 2
            extra = shift_v[...] * rowsum_ref[k * PER_CHUNK + j, r]
            for t in range(thirds):
                block = ordered[q * fold : (q + 1) * fold, t * chans : (t + 1) * chans]
                spec_v[j, t * fold : (t + 1) * fold, r * chans : (r + 1) * chans] = (
                    block * scale_v[1:2, :] + extra
                ).astype(BF16)
        for j in range(PER_CHUNK):
            s = k * PER_CHUNK + j
            coef = dot(leg_v[s], spec_v[j])
            degree = lax.broadcasted_iota(jnp.int32, coef.shape, 0)
            coef = jnp.where(degree >= wave_ref[s], coef, 0.0).astype(BF16)
            mixed = dot(coef, big_v[s]).astype(BF16)
            back = (dot(leg_t_v[s], mixed) * lat_scale).astype(BF16)
            for r in range(2):
                q = 2 * j + r
                for t in range(thirds):
                    z_v[q * fold : (q + 1) * fold, t * chans : (t + 1) * chans] = back[
                        t * fold : (t + 1) * fold, r * chans : (r + 1) * chans
                    ]
        home = dot(one_hot(scatter_ref[...], rows), z_v[...])
        out_two[pl.ds(k * count, count)] = home.reshape(count, GROUP, thirds * chans).astype(BF16)
        in_two[k * count + me] = out_two[k * count + me]
        send_chunk(k, out_two, in_two, recv_two)
        return carry

    lax.fori_loop(0, chunks, middle, 0)

    blocks = 10
    lane_half = (
        lax.broadcasted_iota(jnp.int32, (rows, thirds * chans), 0) // (GROUP // HALVES) % HALVES
    )

    def take(k):
        wait_chunk(k, in_two, recv_two)
        returned = in_two[pl.ds(k * count, count)].reshape(rows, thirds * chans).astype(F32)
        for h in range(HALVES):
            masked_v[h] = jnp.where(lane_half == h, returned, 0.0).astype(BF16)

    take(0)

    def first_block(b, carry):
        at = pl.ds(pl.multiple_of(b * part, 16), part)
        for h in range(HALVES):
            acc_v[h, at, :] = dot(table_t_v[0, at, :], masked_v[h])
        return carry

    lax.fori_loop(0, blocks, first_block, 0)

    def inner(k, carry):
        take(k)

        def block(b, carry):
            at = pl.ds(pl.multiple_of(b * part, 16), part)
            for h in range(HALVES):
                acc_v[h, at, :] += dot(table_t_v[k, at, :], masked_v[h])
            return carry

        return lax.fori_loop(0, blocks, block, carry)

    lax.fori_loop(1, chunks - 1, inner, 0)
    take(chunks - 1)

    def last_block(b, carry):
        at = pl.ds(pl.multiple_of(b * part, 16), part)
        for h in range(HALVES):
            filtered = (acc_v[h, at, :] + dot(table_t_v[chunks - 1, at, :], masked_v[h])) * inv_root
            for t in range(thirds):
                a = h * thirds + t
                normed = (
                    (field_v[a, at, :].astype(F32) - scale_v[0:1, :]) * scale_v[1:2, :]
                ).astype(BF16)
                field_v[a, at, :] = (
                    normed.astype(F32) + filtered[:, t * chans : (t + 1) * chans]
                ).astype(BF16)
        pltpu.make_async_copy(field_v.at[:, at, :], out_hbm.at[:, at, :], store_sem).start()
        return carry

    lax.fori_loop(0, blocks, last_block, 0)
    pltpu.make_async_copy(field_v, out_hbm, store_sem).wait()
    pltpu.make_async_copy(
        stats_v.at[pl.ds(0, count - 1)], stats_v.at[pl.ds(0, count - 1)], stat_sem.at[0]
    ).wait()

    for k in range(2 * chunks):
        sent = in_one.at[pl.ds(0, count - 1)]
        pltpu.make_async_copy(sent, sent, send_sem).wait()


def cosine_rows(waves, width):
    points = np.arange(width, dtype=np.int64)[None, :] * np.arange(waves, dtype=np.int64)[:, None]
    phase = (points % width).astype(np.float32) * np.float32(2.0 * math.pi / width)
    return np.concatenate([np.cos(phase), -np.sin(phase)]).astype(jnp.bfloat16)


def per_device(field, gain, slot_wave, legendre, mixing):
    count = lax.axis_size("lat")
    lat_dev, width, chans = field.shape
    slots, degs, nlat = legendre.shape
    thirds = lat_dev // HALVES
    chunks = slots // PER_CHUNK
    rows = count * GROUP
    fold = HALVES * count
    wide = thirds * chans

    cosines = cosine_rows(degs, width)
    waves = slot_wave.reshape(count, chunks, 1, PER_CHUNK, 1)
    index = waves + degs * jnp.arange(2, dtype=jnp.int32)
    index = jnp.where(waves < degs, index, -1)
    index = jnp.broadcast_to(index, (count, chunks, HALVES, PER_CHUNK, 2))
    index = index.transpose(1, 0, 2, 3, 4).reshape(chunks, 1, rows)
    mine = lax.dynamic_slice_in_dim(slot_wave, lax.axis_index("lat") * slots, slots, 0)
    sums = np.sum(cosines.astype(np.float64), axis=1).astype(np.float32).reshape(2, degs)
    picked = mine[:, None] == jnp.arange(degs, dtype=jnp.int32)[None, :]
    rowsum = jnp.sum(jnp.where(picked[:, None, :], sums[None], 0.0), axis=2)

    d, h, t = np.meshgrid(np.arange(count), np.arange(HALVES), np.arange(thirds), indexing="ij")
    old = (d * lat_dev + h * thirds + t).reshape(-1)
    new = (t * fold + h * count + d).reshape(-1)
    lat_old = np.zeros((1, nlat), np.int32)
    lat_old[0, new] = old
    lat_new = np.zeros((1, nlat), np.int32)
    lat_new[0, old] = new
    d, h, q = np.meshgrid(
        np.arange(count), np.arange(HALVES), np.arange(2 * PER_CHUNK), indexing="ij"
    )
    came = (d * GROUP + h * 2 * PER_CHUNK + q).reshape(-1)
    goes = (q * fold + h * count + d).reshape(-1)
    gather = np.zeros((1, rows), np.int32)
    gather[0, came] = goes
    scatter = np.zeros((1, rows), np.int32)
    scatter[0, goes] = came

    smem = pl.BlockSpec(memory_space=pltpu.SMEM)
    vmem = pl.BlockSpec(memory_space=pltpu.VMEM)
    hbm = pl.BlockSpec(memory_space=pl.ANY)
    parcels = (chunks * count, GROUP, wide)
    return pl.pallas_call(
        functools.partial(layer_kernel, count, float(lat_dev * count * width)),
        out_shape=jax.ShapeDtypeStruct(field.shape, field.dtype),
        in_specs=[smem] * 2 + [vmem] * 6 + [hbm] * 4,
        out_specs=hbm,
        scratch_shapes=[
            pltpu.VMEM(field.shape, BF16),
            pltpu.VMEM((2 * degs, width), BF16),
            pltpu.VMEM(legendre.shape, BF16),
            pltpu.VMEM(mixing.shape, BF16),
            pltpu.VMEM((chunks, rows, width), BF16),
            pltpu.VMEM((chunks, width, rows), BF16),
            pltpu.VMEM(parcels, BF16),
            pltpu.VMEM(parcels, BF16),
            pltpu.VMEM(parcels, BF16),
            pltpu.VMEM(parcels, BF16),
            pltpu.VMEM((slots, degs, nlat), BF16),
            pltpu.VMEM((slots, nlat, degs), BF16),
            pltpu.VMEM((slots, 2 * chans, 2 * chans), BF16),
            pltpu.VMEM((PER_CHUNK, nlat, 2 * chans), BF16),
            pltpu.VMEM((rows, wide), BF16),
            pltpu.VMEM((HALVES, rows, wide), BF16),
            pltpu.VMEM((HALVES, width, wide), F32),
            pltpu.VMEM((2, chans), F32),
            pltpu.VMEM((count, 2, chans), F32),
            pltpu.VMEM((fold, chans), F32),
            pltpu.VMEM((2, chans), F32),
            pltpu.SemaphoreType.DMA,
            pltpu.SemaphoreType.DMA((2,)),
            pltpu.SemaphoreType.DMA((chunks,)),
            pltpu.SemaphoreType.DMA((chunks,)),
            pltpu.SemaphoreType.DMA((4,)),
            pltpu.SemaphoreType.DMA,
        ],
        compiler_params=pltpu.CompilerParams(
            collective_id=0, has_side_effects=True, vmem_limit_bytes=66_000_000
        ),
        name="layer",
    )(
        mine,
        rowsum,
        index,
        jnp.asarray(lat_old),
        jnp.asarray(lat_new),
        jnp.asarray(gather),
        jnp.asarray(scatter),
        gain[None],
        field,
        jnp.asarray(cosines),
        legendre,
        mixing,
    )


def solution(mesh):
    return jax.shard_map(
        per_device,
        mesh=mesh,
        in_specs=(
            P(("member", "lat"), None, None),
            P(),
            P(),
            P("lat", None, None),
            P("lat", None, None, None),
        ),
        out_specs=P(("member", "lat"), None, None),
        check_vma=False,
    )
```

time: 718 us -> 469 us (0.65)
  waiting for transfers between devices: 582 us -> 0 us
  Pallas kernels: 0 us -> 459 us
  starting transfers between devices: 48.2 us -> 0 us
  matrix products: 28.5 us -> 0 us
  other arithmetic: 26.8 us -> 2.06 us
  local copies, waits for them, and re-layouts: 28.5 us -> 7.46 us
    all_to_all x3 -> x0, waiting for transfers between devices: 582 us -> none  [the longest x1 288 us: per_device(): lax.all_to_all(spectrum, 'lat', split_axis=0, concat_axis=1, tiled=True)[0]]
    pallas_call x0 -> x1, Pallas kernels: none -> 459 us  [per_device(): pl.pallas_call(functools.partial(layer_kernel, count, float(lat_dev * cou...]
    all_to_all x3 -> x0, starting transfers between devices: 48.2 us -> none  [the longest x1 34.3 us: from_everyone(): return lax.all_to_all(copies, axis, split_axis=0, concat_axis=0, tiled=True)]
    dot_general x4 -> x0, matrix products: 28.5 us -> none  [the longest x1 9.45 us: per_device(): jnp.einsum('akrc,rkn->anc', returned, inverse, preferred_element_type=jnp...]
    another operation x2 -> x0, other arithmetic: 22.1 us -> none
    reshape x4 -> x3, local copies, waits for them, and re-layouts: 19.7 us -> 1.95 us  [the longest x1 1.1 us: per_device(): index = index.transpose(1, 0, 2, 3, 4).reshape(chunks, 1, rows)]
  transfers between devices with their start and end apart: 3 -> 0, of which waited for: 3 -> 0; matrix products, arithmetic and copies ran while one was open for 3% -> 0% of each run, Pallas kernels for 0% -> 0%
where the time goes in v2:
time: 469 us; the launch traced here: 468 us
  Pallas kernels  459 us (98%)
  local copies, waits for them, and re-layouts  7.46 us (2%)
    pallas_call x1, Pallas kernels, per_device(): pl.pallas_call(functools.partial(layer_kernel, count, float(lat_dev * cou...  459 us

profile of v2, /device:TPU:37, one launch (start us, length us, event | category | flops | bytes accessed | tf_op | source)
XLA Modules:
  0.0 468.4 jit_solution(15097625509306504702)
XLA Ops:
  0.0 0.8 dynamic_slice.3.wave_ref
  0.8 0.0 copy-start
  0.8 0.1 iota_compare_fusion
  0.8 1.4 select_reduce_fusion.rowsum_ref
  2.2 0.8 reshape.45
  3.1 0.6 add_select_fusion
  3.7 0.1 broadcast_bitcast_fusion
  3.8 1.1 reshape.47.index_ref
  4.9 0.0 copy-done
  4.9 458.8 %layer.1 = bf16[6,1440,256]{2,1,0:T(8,128)(2,1)} custom-call(s32[6]{0:T(128)} %copy-done, f32[6,2]{1,0:T(8,128)} %select_reduce_fusion.rowsum_ref, s32[3,1,512]{2,1,0:T(1,128)} %reshape.47.index_ref, s32[1,384]{1,0:T(1,128)} %constant.11.clone.lat_old_ref, s32[1,384]{1,0:T(1,128)} %constant.30.clone.lat_new_ref, s32[1,512]{1,0:T(1,128)} %constant.31.clone.gather_ref, ...), custom_call_target="tpu_custom_call" | custom-call | tf_op jit(solution)/shard_map/layer/pallas_call | solution.py:394
  463.8 4.6 copy.19
  (4 shorter events, 0.1 us)
Async XLA Ops:
  0.8 4.2 copy-start

commit v3 on v2

--- a/solution.py
+++ b/solution.py
@@ -40,7 +40,8 @@
     total_count,
     wave_ref,
     rowsum_ref,
-    index_ref,
+    wave_row_ref,
+    slot_ref,
     lat_old_ref,
     lat_new_ref,
     gather_ref,
@@ -68,9 +69,13 @@
     z_v,
     masked_v,
     acc_v,
+    chosen_v,
     mine_v,
-    stats_v,
-    shift_v,
+    other_v,
+    half_v,
+    halves_v,
+    total_v,
+    rest_v,
     scale_v,
     send_sem,
     stat_sem,
@@ -86,6 +91,9 @@
     chunks = slots // PER_CHUNK
     rows = count * GROUP
     fold = HALVES * count
+    degs_kept = cos_v.shape[0] // 2
+    core = lax.rem(me, 2)
+    partner = me + 1 - 2 * core
     inv_root = 1.0 / math.sqrt(width)
     lat_scale = math.sqrt(nlat / degs)
 
@@ -131,23 +139,29 @@
     squares_here = lax.fori_loop(0, lat_dev * 10, add_squares, jnp.zeros((1, chans), F32))
     mine_v[0:1, :] = mean_here
     mine_v[1:2, :] = squares_here
-    stats_v[me] = mine_v[...]
 
     loads[1].wait()
-
-    def build_table(k, carry):
-        table_v[k] = dot_tn(one_hot(index_ref[k], cos_v.shape[0]), cos_v[...]).astype(BF16)
-        return carry
+    wave_of_slot = one_hot(wave_row_ref[...], degs_kept)
+
+    def build_table(k):
+        for r in range(2):
+            row_slot = one_hot(slot_ref[k, r], wave_row_ref.shape[1])
+            chosen_v[k, r * degs_kept : (r + 1) * degs_kept, :] = dot(wave_of_slot, row_slot).astype(
+                BF16
+            )
+        table_v[k] = dot_tn(chosen_v[k], cos_v[...]).astype(BF16)
 
     row_half = lax.broadcasted_iota(jnp.int32, (rows, chans), 0) // (GROUP // HALVES) % HALVES
 
-    def transform(k):
-        sums = dot(table_v[k], jnp.ones((width, 128), BF16))[:, :1]
+    def transform(k, pivot=None):
+        offset = 0.0
+        if pivot is not None:
+            offset = dot(table_v[k], jnp.ones((width, 128), BF16))[:, :1] * pivot
 
         def third(t, carry):
             low = dot(table_v[k], field_v[t])
             high = dot(table_v[k], field_v[thirds + t])
-            both = (jnp.where(row_half == 0, low, high) - sums * mean_here) * inv_root
+            both = (jnp.where(row_half == 0, low, high) - offset) * inv_root
             out_one[
                 pl.ds(k * count, count), :, pl.ds(pl.multiple_of(t * chans, 128), chans)
             ] = both.reshape(count, GROUP, chans).astype(BF16)
@@ -168,43 +182,87 @@
             ).start()
 
         def both(i, carry):
-            send(lax.rem(me + i, count))
-            send(lax.rem(me + count - i, count))
+            step = jnp.where(lax.rem(i, 2) == 0, count // 2 - 1 - i // 2, (i + 1) // 2)
+            send(lax.rem(me + step, count))
+            send(lax.rem(me + count - step, count))
             return carry
 
-        lax.fori_loop(1, count // 2, both, 0)
+        lax.fori_loop(0, count // 2 - 1, both, 0)
         send(lax.rem(me + count // 2, count))
 
     def wait_chunk(k, dst, recv):
         others = dst.at[pl.ds(k * count, count - 1)]
         pltpu.make_async_copy(others, others, recv.at[k]).wait()
 
-    build_table(0, 0)
-    transform(0)
-    pl.semaphore_wait(barrier, count - 1)
-
-    def send_stats(i, carry):
-        there = lax.rem(me + i, count)
-        pltpu.make_async_remote_copy(
-            src_ref=mine_v,
-            dst_ref=stats_v.at[me],
-            send_sem=stat_sem.at[0],
-            recv_sem=stat_sem.at[1],
+    def tell(src, dst, sems, there):
+        return pltpu.make_async_remote_copy(
+            src_ref=src,
+            dst_ref=dst,
+            send_sem=stat_sem.at[sems],
+            recv_sem=stat_sem.at[sems + 1],
             device_id={"lat": there},
             device_id_type=MESH,
-        ).start()
-        return carry
-
-    lax.fori_loop(1, count, send_stats, 0)
-    send_chunk(0, out_one, in_one, recv_one)
+        )
+
+    build_table(1)
+    transform(1)
+    pl.semaphore_wait(barrier, count - 1)
+
+    lanes = chans // 2
+    pair = tell(mine_v, other_v, 0, partner)
+    pair.start()
+    pair.wait()
+    gap = mine_v[0:1, :] - other_v[0:1, :]
+    pair_mean = (mine_v[0:1, :] + other_v[0:1, :]) * 0.5
+    pair_squares = mine_v[1:2, :] + other_v[1:2, :] + (0.5 * local_count) * gap * gap
+    half_v[0:1, :] = jnp.where(core == 0, pair_mean[:, :lanes], pair_mean[:, lanes:])
+    half_v[1:2, :] = jnp.where(core == 0, pair_squares[:, :lanes], pair_squares[:, lanes:])
+    halves_v[me // 2] = half_v[...]
+
+    def send_stats(i, carry):
+        tell(half_v, halves_v.at[me // 2], 2, lax.rem(me + 2 * i, count)).start()
+        return carry
+
+    lax.fori_loop(1, count // 2, send_stats, 0)
+    send_chunk(1, out_one, in_one, recv_one)
 
     def rest(k, carry):
-        build_table(k, 0)
+        build_table(k)
         transform(k)
         send_chunk(k, out_one, in_one, recv_one)
         return carry
 
-    lax.fori_loop(1, chunks, rest, 0)
+    lax.fori_loop(2, chunks, rest, 0)
+    build_table(0)
+
+    for sem in (2, 3):
+        pltpu.make_async_copy(
+            halves_v.at[pl.ds(0, count // 2 - 1)],
+            halves_v.at[pl.ds(0, count // 2 - 1)],
+            stat_sem.at[sem],
+        ).wait()
+    means = halves_v[:, 0, :]
+    mean_half = jnp.sum(means, axis=0, keepdims=True) / float(count // 2)
+    apart = means - mean_half
+    total_v[0:1, :] = mean_half
+    total_v[1:2, :] = (
+        jnp.sum(halves_v[:, 1, :], axis=0, keepdims=True)
+        + 2.0 * local_count * jnp.sum(apart * apart, axis=0, keepdims=True)
+    ) / total_count
+    share = tell(total_v, rest_v, 4, partner)
+    share.start()
+    share.wait()
+    for i in range(2):
+        scale_v[i : i + 1, :lanes] = jnp.where(
+            core == 0, total_v[i : i + 1, :], rest_v[i : i + 1, :]
+        )
+        scale_v[i : i + 1, lanes:] = jnp.where(
+            core == 0, rest_v[i : i + 1, :], total_v[i : i + 1, :]
+        )
+    mean = scale_v[0:1, :]
+    scale_v[1:2, :] = gain_ref[...] / jnp.sqrt(scale_v[1:2, :] + 1e-05)
+    transform(0, mean)
+    send_chunk(0, out_one, in_one, recv_one)
 
     loads[2].wait()
     loads[3].wait()
@@ -222,40 +280,26 @@
 
     lax.fori_loop(0, slots, prepare, 0)
 
-    waves = cos_v.shape[0] // 2
-    table_row = lax.broadcasted_iota(jnp.int32, (2 * waves, rows), 0)
-    weight = jnp.where((table_row == 0) | (table_row == waves), 1.0, 2.0)
+    table_row = lax.broadcasted_iota(jnp.int32, (2 * degs_kept, rows), 0)
+    weight = jnp.where((table_row == 0) | (table_row == degs_kept), 1.0, 2.0)
 
     def build_table_t(k, carry):
-        chosen = (one_hot(index_ref[k], 2 * waves).astype(F32) * weight).astype(BF16)
+        chosen = (chosen_v[k].astype(F32) * weight).astype(BF16)
         table_t_v[k] = dot_tn(cos_v[...], chosen).astype(BF16)
         return carry
 
     lax.fori_loop(0, chunks, build_table_t, 0)
 
-    pltpu.make_async_copy(
-        stats_v.at[pl.ds(0, count - 1)], stats_v.at[pl.ds(0, count - 1)], stat_sem.at[1]
-    ).wait()
-    means = stats_v[:, 0, :]
-    mean = jnp.sum(means, axis=0, keepdims=True) / float(count)
-    apart = means - mean
-    var = (
-        jnp.sum(stats_v[:, 1, :], axis=0, keepdims=True)
-        + local_count * jnp.sum(apart * apart, axis=0, keepdims=True)
-    ) / total_count
-    scale = gain_ref[...] / jnp.sqrt(var + 1e-05)
-    scale_v[0:1, :] = mean
-    scale_v[1:2, :] = scale
-    for h in range(HALVES):
-        shift_v[h * count : (h + 1) * count, :] = apart * scale * inv_root
-
-    def middle(k, carry):
+    def middle(turn, carry):
+        k = lax.rem(turn + 1, chunks)
         wait_chunk(k, in_one, recv_one)
         arrived = in_one[pl.ds(k * count, count)].reshape(rows, thirds * chans)
         ordered = dot(one_hot(gather_ref[...], rows), arrived)
         for q in range(PER_CHUNK * 2):
             j, r = q // 2, q % 2
-            extra = shift_v[...] * rowsum_ref[k * PER_CHUNK + j, r]
+            wave = jnp.minimum(wave_ref[me * slots + k * PER_CHUNK + j], degs_kept - 1)
+            rowsum = jnp.where(k == 0, 0.0, rowsum_ref[r * degs_kept + wave])
+            extra = scale_v[0:1, :] * scale_v[1:2, :] * (-inv_root * rowsum)
             for t in range(thirds):
                 block = ordered[q * fold : (q + 1) * fold, t * chans : (t + 1) * chans]
                 spec_v[j, t * fold : (t + 1) * fold, r * chans : (r + 1) * chans] = (
@@ -265,7 +309,7 @@
             s = k * PER_CHUNK + j
             coef = dot(leg_v[s], spec_v[j])
             degree = lax.broadcasted_iota(jnp.int32, coef.shape, 0)
-            coef = jnp.where(degree >= wave_ref[s], coef, 0.0).astype(BF16)
+            coef = jnp.where(degree >= wave_ref[me * slots + s], coef, 0.0).astype(BF16)
             mixed = dot(coef, big_v[s]).astype(BF16)
             back = (dot(leg_t_v[s], mixed) * lat_scale).astype(BF16)
             for r in range(2):
@@ -293,12 +337,12 @@
         for h in range(HALVES):
             masked_v[h] = jnp.where(lane_half == h, returned, 0.0).astype(BF16)
 
-    take(0)
+    take(1)
 
     def first_block(b, carry):
         at = pl.ds(pl.multiple_of(b * part, 16), part)
         for h in range(HALVES):
-            acc_v[h, at, :] = dot(table_t_v[0, at, :], masked_v[h])
+            acc_v[h, at, :] = dot(table_t_v[1, at, :], masked_v[h])
         return carry
 
     lax.fori_loop(0, blocks, first_block, 0)
@@ -314,13 +358,13 @@
 
         return lax.fori_loop(0, blocks, block, carry)
 
-    lax.fori_loop(1, chunks - 1, inner, 0)
-    take(chunks - 1)
+    lax.fori_loop(2, chunks, inner, 0)
+    take(0)
 
     def last_block(b, carry):
         at = pl.ds(pl.multiple_of(b * part, 16), part)
         for h in range(HALVES):
-            filtered = (acc_v[h, at, :] + dot(table_t_v[chunks - 1, at, :], masked_v[h])) * inv_root
+            filtered = (acc_v[h, at, :] + dot(table_t_v[0, at, :], masked_v[h])) * inv_root
             for t in range(thirds):
                 a = h * thirds + t
                 normed = (
@@ -334,10 +378,6 @@
 
     lax.fori_loop(0, blocks, last_block, 0)
     pltpu.make_async_copy(field_v, out_hbm, store_sem).wait()
-    pltpu.make_async_copy(
-        stats_v.at[pl.ds(0, count - 1)], stats_v.at[pl.ds(0, count - 1)], stat_sem.at[0]
-    ).wait()
-
     for k in range(2 * chunks):
         sent = in_one.at[pl.ds(0, count - 1)]
         pltpu.make_async_copy(sent, sent, send_sem).wait()
@@ -360,15 +400,18 @@
     wide = thirds * chans
 
     cosines = cosine_rows(degs, width)
-    waves = slot_wave.reshape(count, chunks, 1, PER_CHUNK, 1)
-    index = waves + degs * jnp.arange(2, dtype=jnp.int32)
-    index = jnp.where(waves < degs, index, -1)
-    index = jnp.broadcast_to(index, (count, chunks, HALVES, PER_CHUNK, 2))
-    index = index.transpose(1, 0, 2, 3, 4).reshape(chunks, 1, rows)
-    mine = lax.dynamic_slice_in_dim(slot_wave, lax.axis_index("lat") * slots, slots, 0)
-    sums = np.sum(cosines.astype(np.float64), axis=1).astype(np.float32).reshape(2, degs)
-    picked = mine[:, None] == jnp.arange(degs, dtype=jnp.int32)[None, :]
-    rowsum = jnp.sum(jnp.where(picked[:, None, :], sums[None], 0.0), axis=2)
+    sums = np.sum(cosines.astype(np.float64), axis=1).astype(np.float32)
+    k, r, d, _, j, part = np.meshgrid(
+        np.arange(chunks),
+        np.arange(2),
+        np.arange(count),
+        np.arange(HALVES),
+        np.arange(PER_CHUNK),
+        np.arange(2),
+        indexing="ij",
+    )
+    slot = np.where(r == part, d * slots + k * PER_CHUNK + j, -1).astype(np.int32)
+    slot = slot.reshape(chunks, 2, 1, rows)
 
     d, h, t = np.meshgrid(np.arange(count), np.arange(HALVES), np.arange(thirds), indexing="ij")
     old = (d * lat_dev + h * thirds + t).reshape(-1)
@@ -394,7 +437,7 @@
     return pl.pallas_call(
         functools.partial(layer_kernel, count, float(lat_dev * count * width)),
         out_shape=jax.ShapeDtypeStruct(field.shape, field.dtype),
-        in_specs=[smem] * 2 + [vmem] * 6 + [hbm] * 4,
+        in_specs=[smem] * 2 + [vmem] * 7 + [hbm] * 4,
         out_specs=hbm,
         scratch_shapes=[
             pltpu.VMEM(field.shape, BF16),
@@ -414,12 +457,16 @@
             pltpu.VMEM((rows, wide), BF16),
             pltpu.VMEM((HALVES, rows, wide), BF16),
             pltpu.VMEM((HALVES, width, wide), F32),
+            pltpu.VMEM((chunks, 2 * degs, rows), BF16),
             pltpu.VMEM((2, chans), F32),
-            pltpu.VMEM((count, 2, chans), F32),
-            pltpu.VMEM((fold, chans), F32),
+            pltpu.VMEM((2, chans), F32),
+            pltpu.VMEM((2, chans // 2), F32),
+            pltpu.VMEM((count // 2, 2, chans // 2), F32),
+            pltpu.VMEM((2, chans // 2), F32),
+            pltpu.VMEM((2, chans // 2), F32),
             pltpu.VMEM((2, chans), F32),
             pltpu.SemaphoreType.DMA,
-            pltpu.SemaphoreType.DMA((2,)),
+            pltpu.SemaphoreType.DMA((6,)),
             pltpu.SemaphoreType.DMA((chunks,)),
             pltpu.SemaphoreType.DMA((chunks,)),
             pltpu.SemaphoreType.DMA((4,)),
@@ -430,9 +477,10 @@
         ),
         name="layer",
     )(
-        mine,
-        rowsum,
-        index,
+        slot_wave,
+        jnp.asarray(sums),
+        slot_wave[None],
+        jnp.asarray(slot),
         jnp.asarray(lat_old),
         jnp.asarray(lat_new),
         jnp.asarray(gather),

time: 469 us -> 462 us (0.985)
  Pallas kernels: 459 us -> 454 us
    pallas_call x1, Pallas kernels: 459 us -> 454 us  [per_device(): pl.pallas_call(functools.partial(layer_kernel, count, float(lat_dev * cou...]
where the time goes in v3:
time: 462 us; the launch traced here: 460 us
  Pallas kernels  454 us (98%)
  local copies, waits for them, and re-layouts  5.87 us (1%)
    pallas_call x1, Pallas kernels, per_device(): pl.pallas_call(functools.partial(layer_kernel, count, float(lat_dev * cou...  454 us

profile of v3, /device:TPU:37, one launch (start us, length us, event | category | flops | bytes accessed | tf_op | source)
XLA Modules:
  0.0 459.5 jit_solution(17922100486793917402)
XLA Ops:
  0.0 1.2 broadcast_in_dim.6.wave_row_ref
  1.2 453.7 %layer.1 = bf16[6,1440,256]{2,1,0:T(8,128)(2,1)} custom-call(s32[384]{0:T(512)} %wave_ref.1, f32[768]{0:T(1024)} %constant.14.clone.rowsum_ref, s32[1,384]{1,0:T(1,128)} %broadcast_in_dim.6.wave_row_ref, s32[3,2,1,512]{3,2,1,0:T(1,128)} %constant.15.clone.slot_ref, s32[1,384]{1,0:T(1,128)} %constant.16.clone.lat_old_ref, ...), custom_call_target="tpu_custom_call" | custom-call | tf_op jit(solution)/shard_map/layer/pallas_call | solution.py:437
  454.9 4.6 %copy.14 = bf16[6,1440,256]{2,1,0:T(8,128)(2,1)} copy(bf16[6,1440,256]{2,1,0:T(8,128)(2,1)} %layer.1) | data formatting | bytes 8847360

commit v4 on v3

--- a/solution.py
+++ b/solution.py
@@ -15,6 +15,8 @@
 HALVES = 2
 PER_CHUNK = 2
 GROUP = HALVES * PER_CHUNK * 2
+HUB_LATS = 128
+SIDES = (1, -1)
 
 
 def dot(a, b):
@@ -46,6 +48,11 @@
     lat_new_ref,
     gather_ref,
     scatter_ref,
+    hub_chip_ref,
+    hub_inner_ref,
+    hub_lane_ref,
+    hub_gather_ref,
+    hub_scatter_ref,
     gain_ref,
     field_hbm,
     cos_hbm,
@@ -70,6 +77,18 @@
     masked_v,
     acc_v,
     chosen_v,
+    hub_in,
+    hub_out,
+    leg_out,
+    leg_in,
+    part_out,
+    part_in,
+    mix_out,
+    mix_in,
+    coef_v,
+    mixed_v,
+    hub_spec_v,
+    hub_z_v,
     mine_v,
     other_v,
     half_v,
@@ -81,6 +100,10 @@
     stat_sem,
     recv_one,
     recv_two,
+    hub_sem,
+    leg_sem,
+    part_sem,
+    mix_sem,
     load_sem,
     store_sem,
 ):
@@ -94,6 +117,19 @@
     degs_kept = cos_v.shape[0] // 2
     core = lax.rem(me, 2)
     partner = me + 1 - 2 * core
+    chip = me // 2
+    chips = count // 2
+    far = chips // 2
+    served = hub_in.shape[1]
+    reach = far - (served - 1) // 2
+    packed = part_in.shape[1]
+    hub_fold = hub_spec_v.shape[1] // thirds
+    last = chunks - 1
+    near = 2 * (2 * reach - 1)
+
+    def device(at_chip, at_core):
+        return 2 * lax.rem(at_chip + 2 * chips, chips) + at_core
+
     inv_root = 1.0 / math.sqrt(width)
     lat_scale = math.sqrt(nlat / degs)
 
@@ -105,6 +141,7 @@
         )
         return carry
 
+    in_one[last * count : (last + 1) * count] = jnp.zeros((count, *in_one.shape[1:]), BF16)
     lax.fori_loop(1, count, greet, 0)
 
     loads = [
@@ -153,10 +190,8 @@
 
     row_half = lax.broadcasted_iota(jnp.int32, (rows, chans), 0) // (GROUP // HALVES) % HALVES
 
-    def transform(k, pivot=None):
-        offset = 0.0
-        if pivot is not None:
-            offset = dot(table_v[k], jnp.ones((width, 128), BF16))[:, :1] * pivot
+    def transform(k):
+        offset = dot(table_v[k], jnp.ones((width, 128), BF16))[:, :1] * scale_v[0:1, :]
 
         def third(t, carry):
             low = dot(table_v[k], field_v[t])
@@ -168,7 +203,107 @@
             return carry
 
         lax.fori_loop(0, thirds, third, 0)
-        in_one[k * count + me] = out_one[k * count + me]
+
+    def parcel(src, dst, there, recv):
+        pltpu.make_async_remote_copy(
+            src_ref=src,
+            dst_ref=dst,
+            send_sem=send_sem,
+            recv_sem=recv,
+            device_id={"lat": there},
+            device_id_type=MESH,
+        ).start()
+
+    def send_near(src, dst, recv):
+        first = device(chip - (reach - 1), 0)
+
+        def send(i, carry):
+            step = lax.rem(2 * (reach - 1) + core + i, near)
+            there = lax.rem(first + step, count)
+            parcel(src.at[last * count + there], dst.at[last * count + me], there, recv.at[last])
+            return carry
+
+        lax.fori_loop(1, near, send, 0)
+
+    def send_to_hubs():
+        def block(owner):
+            return out_one.at[last * count + owner]
+
+        side_here = 1 - 2 * core
+        for to in range(2):
+            there = device(chip - side_here * (far - reach), to)
+            parcel(
+                block(device(chip + far, to)),
+                hub_in.at[core, served - 1],
+                there,
+                hub_sem.at[core],
+            )
+        for i, side in enumerate(SIDES):
+
+            def send(v, carry):
+                e, to = v // 2, lax.rem(v, 2)
+                parcel(
+                    block(device(chip - side * (e + reach), to)),
+                    hub_in.at[i, 2 * e + core],
+                    device(chip - side * e, to),
+                    hub_sem.at[i],
+                )
+                return carry
+
+            lax.fori_loop(2, served - 1, send, 0)
+            parcel(
+                block(device(chip - side * reach, 1 - core)),
+                hub_in.at[i, core],
+                partner,
+                hub_sem.at[i],
+            )
+            hub_in[i, core] = out_one[last * count + device(chip - side * reach, core)]
+
+    def send_from_hub(i):
+        side = SIDES[i]
+        owner = device(chip - side * reach, core)
+        dst = in_two.at[last * count + owner]
+
+        def send(v, carry):
+            there = device(chip + side * (v // 2), lax.rem(v, 2))
+            parcel(hub_out.at[i, v], dst, there, recv_two.at[last])
+            return carry
+
+        lax.fori_loop(2, served - 1, send, 0)
+        parcel(hub_out.at[i, 1 - core], dst, partner, recv_two.at[last])
+        there = device(chip + side * (far - reach), i)
+        parcel(hub_out.at[i, served - 1], dst, there, recv_two.at[last])
+        in_two[last * count + owner] = hub_out[i, core]
+
+    def to_side(src, dst, sems, i, toward):
+        return pltpu.make_async_remote_copy(
+            src_ref=src,
+            dst_ref=dst.at[i],
+            send_sem=sems.at[i],
+            recv_sem=sems.at[2 + i],
+            device_id={"lat": device(chip + toward * SIDES[i] * reach, core)},
+            device_id_type=MESH,
+        )
+
+    def wave_at(owner, j):
+        return wave_ref[owner * slots + last * PER_CHUNK + j]
+
+    def pack(owner, j):
+        low = degs - wave_at(owner, 0)
+        begin = jnp.where(j == 0, 0, low)
+        end = begin + degs - wave_at(owner, j)
+        degree = lax.broadcasted_iota(jnp.int32, (degs, packed), 0)
+        row = lax.broadcasted_iota(jnp.int32, (degs, packed), 1)
+        hit = (degree - row == wave_at(owner, j) - begin) & (row >= begin) & (row < end)
+        return jnp.where(hit, 1.0, 0.0).astype(BF16)
+
+    def hub_legendre(i):
+        return dot(leg_in[i], one_hot(hub_lane_ref[...], HUB_LATS)).astype(BF16)
+
+    def of_slot(i, j, value):
+        low = degs - wave_at(device(chip - SIDES[i] * reach, core), 0)
+        row = lax.broadcasted_iota(jnp.int32, value.shape, 0)
+        return jnp.where((row < low) == (j == 0), value, 0.0)
 
     def send_chunk(k, src, dst, recv):
         def send(there):
@@ -190,8 +325,8 @@
         lax.fori_loop(0, count // 2 - 1, both, 0)
         send(lax.rem(me + count // 2, count))
 
-    def wait_chunk(k, dst, recv):
-        others = dst.at[pl.ds(k * count, count - 1)]
+    def wait_chunk(k, dst, recv, parcels):
+        others = dst.at[pl.ds(k * count, parcels)]
         pltpu.make_async_copy(others, others, recv.at[k]).wait()
 
     def tell(src, dst, sems, there):
@@ -204,11 +339,76 @@
             device_id_type=MESH,
         )
 
-    build_table(1)
-    transform(1)
+    lanes = chans // 2
+    def normalise(block, owner, k, j, r, keep):
+        wave = jnp.minimum(wave_ref[owner * slots + k * PER_CHUNK + j], degs_kept - 1)
+        rowsum = jnp.where(k == 0, 0.0, rowsum_ref[r * degs_kept + wave])
+        extra = scale_v[0:1, :] * scale_v[1:2, :] * (-inv_root * rowsum)
+        return (block * scale_v[1:2, :] + extra * keep).astype(BF16)
+
+    def hub_forward():
+        for sem in (2, 3):
+            pltpu.make_async_copy(
+                halves_v.at[pl.ds(0, count // 2 - 1)],
+                halves_v.at[pl.ds(0, count // 2 - 1)],
+                stat_sem.at[sem],
+            ).wait()
+        means = halves_v[:, 0, :]
+        mean_half = jnp.sum(means, axis=0, keepdims=True) / float(count // 2)
+        apart = means - mean_half
+        total_v[0:1, :] = mean_half
+        total_v[1:2, :] = (
+            jnp.sum(halves_v[:, 1, :], axis=0, keepdims=True)
+            + 2.0 * local_count * jnp.sum(apart * apart, axis=0, keepdims=True)
+        ) / total_count
+        share = tell(total_v, rest_v, 4, partner)
+        share.start()
+        share.wait()
+        for i in range(2):
+            scale_v[i : i + 1, :lanes] = jnp.where(
+                core == 0, total_v[i : i + 1, :], rest_v[i : i + 1, :]
+            )
+            scale_v[i : i + 1, lanes:] = jnp.where(
+                core == 0, rest_v[i : i + 1, :], total_v[i : i + 1, :]
+            )
+        scale_v[1:2, :] = gain_ref[...] / jnp.sqrt(scale_v[1:2, :] + 1e-05)
+
+        for i in range(2):
+            to_side(leg_out.at[i], leg_in, leg_sem, i, 1).wait()
+            pltpu.make_async_copy(
+                hub_in.at[i, pl.ds(0, served - 1)], hub_in.at[i, pl.ds(0, served - 1)], hub_sem.at[i]
+            ).wait()
+            owner = device(chip - SIDES[i] * reach, core)
+            arrived = hub_in[i].reshape(served * GROUP, thirds * chans)
+            ordered = dot(one_hot(hub_gather_ref[...], 2 * PER_CHUNK * hub_fold), arrived)
+            for q in range(2 * PER_CHUNK):
+                j, r = q // 2, q % 2
+                for t in range(thirds):
+                    block = ordered[q * hub_fold : (q + 1) * hub_fold, t * chans : (t + 1) * chans]
+                    hub_spec_v[j, t * hub_fold : (t + 1) * hub_fold, r * chans : (r + 1) * chans] = (
+                        normalise(block, owner, last, j, r, 1.0)
+                    )
+            leg = hub_legendre(i)
+            total = of_slot(i, 0, dot(leg, hub_spec_v[0])) + of_slot(i, 1, dot(leg, hub_spec_v[1]))
+            part_out[i] = total.astype(BF16)
+            to_side(part_out.at[i], part_in, part_sem, i, -1).start()
+
+    scale_v[...] = jnp.zeros_like(scale_v)
+    acc_v[...] = jnp.zeros_like(acc_v)
+
+    build_table(last)
+    transform(last)
+    loads[2].wait()
+    for i, side in enumerate(SIDES):
+        at_chip = lax.rem(chip + side * hub_chip_ref[...] + 2 * chips, chips)
+        lats = one_hot(at_chip * (2 * lat_dev) + hub_inner_ref[i], nlat)
+        rows_here = jnp.zeros((packed, HUB_LATS), F32)
+        for j in range(PER_CHUNK):
+            values = dot(legendre_v[last * PER_CHUNK + j], lats).astype(BF16)
+            rows_here += dot_tn(pack(me, j), values)
+        leg_out[i] = rows_here.astype(BF16)
     pl.semaphore_wait(barrier, count - 1)
 
-    lanes = chans // 2
     pair = tell(mine_v, other_v, 0, partner)
     pair.start()
     pair.wait()
@@ -224,47 +424,23 @@
         return carry
 
     lax.fori_loop(1, count // 2, send_stats, 0)
-    send_chunk(1, out_one, in_one, recv_one)
-
-    def rest(k, carry):
+    for i in range(2):
+        to_side(leg_out.at[i], leg_in, leg_sem, i, 1).start()
+    send_to_hubs()
+    send_near(out_one, in_one, recv_one)
+    in_one[last * count + me] = out_one[last * count + me]
+
+    def outward(turn, carry):
+        k = last - turn
         build_table(k)
+        pl.when(k == 0)(hub_forward)
         transform(k)
         send_chunk(k, out_one, in_one, recv_one)
+        in_one[k * count + me] = out_one[k * count + me]
         return carry
 
-    lax.fori_loop(2, chunks, rest, 0)
-    build_table(0)
-
-    for sem in (2, 3):
-        pltpu.make_async_copy(
-            halves_v.at[pl.ds(0, count // 2 - 1)],
-            halves_v.at[pl.ds(0, count // 2 - 1)],
-            stat_sem.at[sem],
-        ).wait()
-    means = halves_v[:, 0, :]
-    mean_half = jnp.sum(means, axis=0, keepdims=True) / float(count // 2)
-    apart = means - mean_half
-    total_v[0:1, :] = mean_half
-    total_v[1:2, :] = (
-        jnp.sum(halves_v[:, 1, :], axis=0, keepdims=True)
-        + 2.0 * local_count * jnp.sum(apart * apart, axis=0, keepdims=True)
-    ) / total_count
-    share = tell(total_v, rest_v, 4, partner)
-    share.start()
-    share.wait()
-    for i in range(2):
-        scale_v[i : i + 1, :lanes] = jnp.where(
-            core == 0, total_v[i : i + 1, :], rest_v[i : i + 1, :]
-        )
-        scale_v[i : i + 1, lanes:] = jnp.where(
-            core == 0, rest_v[i : i + 1, :], total_v[i : i + 1, :]
-        )
-    mean = scale_v[0:1, :]
-    scale_v[1:2, :] = gain_ref[...] / jnp.sqrt(scale_v[1:2, :] + 1e-05)
-    transform(0, mean)
-    send_chunk(0, out_one, in_one, recv_one)
-
-    loads[2].wait()
+    lax.fori_loop(1, chunks, outward, 0)
+
     loads[3].wait()
 
     def prepare(s, carry):
@@ -290,38 +466,93 @@
 
     lax.fori_loop(0, chunks, build_table_t, 0)
 
+    place = lax.rem(lax.broadcasted_iota(jnp.int32, (fold, chans), 0), count) // 2
+    apart_chips = jnp.abs(place - chip)
+    close = jnp.minimum(apart_chips, chips - apart_chips) < reach
+
     def middle(turn, carry):
-        k = lax.rem(turn + 1, chunks)
-        wait_chunk(k, in_one, recv_one)
+        k = last - turn
+
+        @pl.when(k == last)
+        def _():
+            wait_chunk(last, in_one, recv_one, near - 1)
+            for i in range(2):
+                to_side(part_out.at[i], part_in, part_sem, i, -1).wait()
+
+        @pl.when(k == 0)
+        def _():
+            for i in range(2):
+                to_side(mix_out, mix_in, mix_sem, i, 1).wait()
+                leg = hub_legendre(i)
+                for j in range(PER_CHUNK):
+                    rows_j = of_slot(i, j, mix_in[i].astype(F32)).astype(BF16)
+                    back = (dot_tn(leg, rows_j) * lat_scale).astype(BF16)
+                    for r in range(2):
+                        q = 2 * j + r
+                        for t in range(thirds):
+                            hub_z_v[
+                                q * hub_fold : (q + 1) * hub_fold, t * chans : (t + 1) * chans
+                            ] = back[t * hub_fold : (t + 1) * hub_fold, r * chans : (r + 1) * chans]
+                home = dot(one_hot(hub_scatter_ref[...], served * GROUP), hub_z_v[...])
+                hub_out[i] = home.reshape(served, GROUP, thirds * chans).astype(BF16)
+                send_from_hub(i)
+
+        @pl.when(k != last)
+        def _():
+            wait_chunk(k, in_one, recv_one, count - 1)
+
         arrived = in_one[pl.ds(k * count, count)].reshape(rows, thirds * chans)
         ordered = dot(one_hot(gather_ref[...], rows), arrived)
+        keep = jnp.where(close | (k != last), 1.0, 0.0)
         for q in range(PER_CHUNK * 2):
             j, r = q // 2, q % 2
-            wave = jnp.minimum(wave_ref[me * slots + k * PER_CHUNK + j], degs_kept - 1)
-            rowsum = jnp.where(k == 0, 0.0, rowsum_ref[r * degs_kept + wave])
-            extra = scale_v[0:1, :] * scale_v[1:2, :] * (-inv_root * rowsum)
             for t in range(thirds):
                 block = ordered[q * fold : (q + 1) * fold, t * chans : (t + 1) * chans]
-                spec_v[j, t * fold : (t + 1) * fold, r * chans : (r + 1) * chans] = (
-                    block * scale_v[1:2, :] + extra
-                ).astype(BF16)
-        for j in range(PER_CHUNK):
+                spec_v[j, t * fold : (t + 1) * fold, r * chans : (r + 1) * chans] = normalise(
+                    block, me, k, j, r, keep
+                )
+
+        def one_slot(j, carry):
             s = k * PER_CHUNK + j
-            coef = dot(leg_v[s], spec_v[j])
-            degree = lax.broadcasted_iota(jnp.int32, coef.shape, 0)
-            coef = jnp.where(degree >= wave_ref[me * slots + s], coef, 0.0).astype(BF16)
-            mixed = dot(coef, big_v[s]).astype(BF16)
-            back = (dot(leg_t_v[s], mixed) * lat_scale).astype(BF16)
+            coef_v[...] = dot(leg_v[s], spec_v[j])
+
+            @pl.when(k == last)
+            def _():
+                for i in range(2):
+                    coef_v[...] += dot(pack(me, j), part_in[i])
+
+            degree = lax.broadcasted_iota(jnp.int32, coef_v.shape, 0)
+            coef = jnp.where(degree >= wave_ref[me * slots + s], coef_v[...], 0.0).astype(BF16)
+            mixed_v[j] = dot(coef, big_v[s]).astype(BF16)
+            back = (dot(leg_t_v[s], mixed_v[j]) * lat_scale).astype(BF16)
             for r in range(2):
                 q = 2 * j + r
                 for t in range(thirds):
-                    z_v[q * fold : (q + 1) * fold, t * chans : (t + 1) * chans] = back[
+                    z_v[
+                        pl.ds(pl.multiple_of(q * fold, 16), fold), t * chans : (t + 1) * chans
+                    ] = back[
                         t * fold : (t + 1) * fold, r * chans : (r + 1) * chans
                     ]
+            return carry
+
+        lax.fori_loop(0, PER_CHUNK, one_slot, 0)
         home = dot(one_hot(scatter_ref[...], rows), z_v[...])
         out_two[pl.ds(k * count, count)] = home.reshape(count, GROUP, thirds * chans).astype(BF16)
         in_two[k * count + me] = out_two[k * count + me]
-        send_chunk(k, out_two, in_two, recv_two)
+
+        @pl.when(k == last)
+        def _():
+            mix_out[...] = (
+                dot_tn(pack(me, 0), mixed_v[0]) + dot_tn(pack(me, 1), mixed_v[1])
+            ).astype(BF16)
+            for i in range(2):
+                to_side(mix_out, mix_in, mix_sem, i, 1).start()
+            send_near(out_two, in_two, recv_two)
+
+        @pl.when(k != last)
+        def _():
+            send_chunk(k, out_two, in_two, recv_two)
+
         return carry
 
     lax.fori_loop(0, chunks, middle, 0)
@@ -332,54 +563,48 @@
     )
 
     def take(k):
-        wait_chunk(k, in_two, recv_two)
         returned = in_two[pl.ds(k * count, count)].reshape(rows, thirds * chans).astype(F32)
         for h in range(HALVES):
             masked_v[h] = jnp.where(lane_half == h, returned, 0.0).astype(BF16)
 
-    take(1)
-
-    def first_block(b, carry):
-        at = pl.ds(pl.multiple_of(b * part, 16), part)
-        for h in range(HALVES):
-            acc_v[h, at, :] = dot(table_t_v[1, at, :], masked_v[h])
+    def inner(turn, carry):
+        k = last - turn
+        pl.when(k == last)(lambda: wait_chunk(last, in_two, recv_two, count - 3))
+        pl.when(k != last)(lambda: wait_chunk(k, in_two, recv_two, count - 1))
+        take(k)
+
+        def block(i, carry):
+            h = i // blocks
+            at = pl.ds(pl.multiple_of(lax.rem(i, blocks) * part, 16), part)
+            acc_v[h, at, :] += dot(table_t_v[k, at, :], masked_v[h])
+            return carry
+
+        return lax.fori_loop(0, HALVES * blocks, block, carry)
+
+    lax.fori_loop(0, chunks - 1, inner, 0)
+    wait_chunk(0, in_two, recv_two, count - 1)
+    take(0)
+
+    def last_block(i, carry):
+        h = i // blocks
+        at = pl.ds(pl.multiple_of(lax.rem(i, blocks) * part, 16), part)
+        filtered = (acc_v[h, at, :] + dot(table_t_v[0, at, :], masked_v[h])) * inv_root
+        for t in range(thirds):
+            a = h * thirds + t
+            normed = (
+                (field_v[a, at, :].astype(F32) - scale_v[0:1, :]) * scale_v[1:2, :]
+            ).astype(BF16)
+            field_v[a, at, :] = (
+                normed.astype(F32) + filtered[:, t * chans : (t + 1) * chans]
+            ).astype(BF16)
+        these = pl.ds(h * thirds, thirds)
+        pltpu.make_async_copy(field_v.at[these, at, :], out_hbm.at[these, at, :], store_sem).start()
         return carry
 
-    lax.fori_loop(0, blocks, first_block, 0)
-
-    def inner(k, carry):
-        take(k)
-
-        def block(b, carry):
-            at = pl.ds(pl.multiple_of(b * part, 16), part)
-            for h in range(HALVES):
-                acc_v[h, at, :] += dot(table_t_v[k, at, :], masked_v[h])
-            return carry
-
-        return lax.fori_loop(0, blocks, block, carry)
-
-    lax.fori_loop(2, chunks, inner, 0)
-    take(0)
-
-    def last_block(b, carry):
-        at = pl.ds(pl.multiple_of(b * part, 16), part)
-        for h in range(HALVES):
-            filtered = (acc_v[h, at, :] + dot(table_t_v[0, at, :], masked_v[h])) * inv_root
-            for t in range(thirds):
-                a = h * thirds + t
-                normed = (
-                    (field_v[a, at, :].astype(F32) - scale_v[0:1, :]) * scale_v[1:2, :]
-                ).astype(BF16)
-                field_v[a, at, :] = (
-                    normed.astype(F32) + filtered[:, t * chans : (t + 1) * chans]
-                ).astype(BF16)
-        pltpu.make_async_copy(field_v.at[:, at, :], out_hbm.at[:, at, :], store_sem).start()
-        return carry
-
-    lax.fori_loop(0, blocks, last_block, 0)
+    lax.fori_loop(0, HALVES * blocks, last_block, 0)
     pltpu.make_async_copy(field_v, out_hbm, store_sem).wait()
-    for k in range(2 * chunks):
-        sent = in_one.at[pl.ds(0, count - 1)]
+    for amount in [count - 1] * (2 * last) + [near - 1, 2 * (served - 1)] * 2:
+        sent = in_one.at[pl.ds(0, amount)]
         pltpu.make_async_copy(sent, sent, send_sem).wait()
 
 
@@ -430,6 +655,35 @@
     scatter = np.zeros((1, rows), np.int32)
     scatter[0, goes] = came
 
+    far = count // 4
+    served = 2 * (far - 2) + 1
+    while served * lat_dev > HUB_LATS:
+        served -= 2
+    reach = far - (served - 1) // 2
+    hub_fold = HALVES * (-(-served // 8) * 8)
+    packed = -(-(2 * degs - (4 * (chunks - 1) + 2) * count + 1) // 8) * 8
+    t, h, p = np.meshgrid(
+        np.arange(thirds), np.arange(HALVES), np.arange(served), indexing="ij"
+    )
+    lane = np.arange(t.size)
+    hub_chip = np.zeros((1, HUB_LATS), np.int32)
+    hub_chip[0, lane] = (reach + p // 2).reshape(-1)
+    hub_inner = np.full((2, 1, HUB_LATS), -(2**20), np.int32)
+    for i in range(2):
+        at_core = np.where(p == served - 1, i, p % 2)
+        hub_inner[i, 0, lane] = (at_core * lat_dev + h * thirds + t).reshape(-1)
+    hub_lane = np.full((1, thirds * hub_fold), -1, np.int32)
+    hub_lane[0, (t * hub_fold + h * (hub_fold // HALVES) + p).reshape(-1)] = lane
+    p, h, q = np.meshgrid(
+        np.arange(served), np.arange(HALVES), np.arange(2 * PER_CHUNK), indexing="ij"
+    )
+    came = (p * GROUP + h * 2 * PER_CHUNK + q).reshape(-1)
+    goes = (q * hub_fold + h * (hub_fold // HALVES) + p).reshape(-1)
+    hub_gather = np.zeros((1, served * GROUP), np.int32)
+    hub_gather[0, came] = goes
+    hub_scatter = np.full((1, 2 * PER_CHUNK * hub_fold), -1, np.int32)
+    hub_scatter[0, goes] = came
+
     smem = pl.BlockSpec(memory_space=pltpu.SMEM)
     vmem = pl.BlockSpec(memory_space=pltpu.VMEM)
     hbm = pl.BlockSpec(memory_space=pl.ANY)
@@ -437,7 +691,7 @@
     return pl.pallas_call(
         functools.partial(layer_kernel, count, float(lat_dev * count * width)),
         out_shape=jax.ShapeDtypeStruct(field.shape, field.dtype),
-        in_specs=[smem] * 2 + [vmem] * 7 + [hbm] * 4,
+        in_specs=[smem] * 2 + [vmem] * 12 + [hbm] * 4,
         out_specs=hbm,
         scratch_shapes=[
             pltpu.VMEM(field.shape, BF16),
@@ -458,6 +712,18 @@
             pltpu.VMEM((HALVES, rows, wide), BF16),
             pltpu.VMEM((HALVES, width, wide), F32),
             pltpu.VMEM((chunks, 2 * degs, rows), BF16),
+            pltpu.VMEM((2, served, GROUP, wide), BF16),
+            pltpu.VMEM((2, served, GROUP, wide), BF16),
+            pltpu.VMEM((2, packed, HUB_LATS), BF16),
+            pltpu.VMEM((2, packed, HUB_LATS), BF16),
+            pltpu.VMEM((2, packed, 2 * chans), BF16),
+            pltpu.VMEM((2, packed, 2 * chans), BF16),
+            pltpu.VMEM((packed, 2 * chans), BF16),
+            pltpu.VMEM((2, packed, 2 * chans), BF16),
+            pltpu.VMEM((degs, 2 * chans), F32),
+            pltpu.VMEM((PER_CHUNK, degs, 2 * chans), BF16),
+            pltpu.VMEM((PER_CHUNK, thirds * hub_fold, 2 * chans), BF16),
+            pltpu.VMEM((2 * PER_CHUNK * hub_fold, wide), BF16),
             pltpu.VMEM((2, chans), F32),
             pltpu.VMEM((2, chans), F32),
             pltpu.VMEM((2, chans // 2), F32),
@@ -469,6 +735,10 @@
             pltpu.SemaphoreType.DMA((6,)),
             pltpu.SemaphoreType.DMA((chunks,)),
             pltpu.SemaphoreType.DMA((chunks,)),
+            pltpu.SemaphoreType.DMA((2,)),
+            pltpu.SemaphoreType.DMA((4,)),
+            pltpu.SemaphoreType.DMA((4,)),
+            pltpu.SemaphoreType.DMA((4,)),
             pltpu.SemaphoreType.DMA((4,)),
             pltpu.SemaphoreType.DMA,
         ],
@@ -485,6 +755,11 @@
         jnp.asarray(lat_new),
         jnp.asarray(gather),
         jnp.asarray(scatter),
+        jnp.asarray(hub_chip),
+        jnp.asarray(hub_inner),
+        jnp.asarray(hub_lane),
+        jnp.asarray(hub_gather),
+        jnp.asarray(hub_scatter),
         gain[None],
         field,
         jnp.asarray(cosines),

time: 462 us -> 442 us (0.957)
  Pallas kernels: 454 us -> 436 us
    pallas_call x1, Pallas kernels: 454 us -> 436 us  [per_device(): pl.pallas_call(functools.partial(layer_kernel, count, float(lat_dev * cou...]
where the time goes in v4:
time: 442 us
  Pallas kernels  436 us (99%)
  local copies, waits for them, and re-layouts  5.87 us (1%)
    pallas_call x1, Pallas kernels, per_device(): pl.pallas_call(functools.partial(layer_kernel, count, float(lat_dev * cou...  436 us

profile of v4, /device:TPU:37, one launch (start us, length us, event | category | flops | bytes accessed | tf_op | source)
XLA Modules:
  0.0 442.2 jit_solution(9445300908407965582)
XLA Ops:
  0.0 1.2 broadcast_in_dim.6.wave_row_ref
  1.2 436.3 %layer.1 = bf16[6,1440,256]{2,1,0:T(8,128)(2,1)} custom-call(s32[384]{0:T(512)} %wave_ref.1, f32[768]{0:T(1024)} %constant.24.clone.rowsum_ref, s32[1,384]{1,0:T(1,128)} %broadcast_in_dim.6.wave_row_ref, s32[3,2,1,512]{3,2,1,0:T(1,128)} %constant.25.clone.slot_ref, s32[1,384]{1,0:T(1,128)} %constant.26.clone.lat_old_ref, ...), custom_call_target="tpu_custom_call" | custom-call | tf_op jit(solution)/shard_map/layer/pallas_call | solution.py:691
  437.5 4.6 %copy.19 = bf16[6,1440,256]{2,1,0:T(8,128)(2,1)} copy(bf16[6,1440,256]{2,1,0:T(8,128)(2,1)} %layer.1) | data formatting | bytes 8847360

commit v5 on v4

--- a/solution.py
+++ b/solution.py
@@ -16,7 +16,6 @@
 PER_CHUNK = 2
 GROUP = HALVES * PER_CHUNK * 2
 HUB_LATS = 128
-SIDES = (1, -1)
 
 
 def dot(a, b):
@@ -53,6 +52,8 @@
     hub_lane_ref,
     hub_gather_ref,
     hub_scatter_ref,
+    pick_ref,
+    single_ref,
     gain_ref,
     field_hbm,
     cos_hbm,
@@ -74,7 +75,7 @@
     big_v,
     spec_v,
     z_v,
-    masked_v,
+    picked_v,
     acc_v,
     chosen_v,
     hub_in,
@@ -178,11 +179,11 @@
     mine_v[1:2, :] = squares_here
 
     loads[1].wait()
-    wave_of_slot = one_hot(wave_row_ref[...], degs_kept)
+    wave_of_slot = one_hot(wave_row_ref[...][None, :], degs_kept)
 
     def build_table(k):
         for r in range(2):
-            row_slot = one_hot(slot_ref[k, r], wave_row_ref.shape[1])
+            row_slot = one_hot(slot_ref[k, r], wave_row_ref.shape[0])
             chosen_v[k, r * degs_kept : (r + 1) * degs_kept, :] = dot(wave_of_slot, row_slot).astype(
                 BF16
             )
@@ -238,7 +239,7 @@
                 there,
                 hub_sem.at[core],
             )
-        for i, side in enumerate(SIDES):
+        for i, side in enumerate((1, -1)):
 
             def send(v, carry):
                 e, to = v // 2, lax.rem(v, 2)
@@ -260,7 +261,7 @@
             hub_in[i, core] = out_one[last * count + device(chip - side * reach, core)]
 
     def send_from_hub(i):
-        side = SIDES[i]
+        side = 1 - 2 * i
         owner = device(chip - side * reach, core)
         dst = in_two.at[last * count + owner]
 
@@ -281,7 +282,7 @@
             dst_ref=dst.at[i],
             send_sem=sems.at[i],
             recv_sem=sems.at[2 + i],
-            device_id={"lat": device(chip + toward * SIDES[i] * reach, core)},
+            device_id={"lat": device(chip + toward * (1 - 2 * i) * reach, core)},
             device_id_type=MESH,
         )
 
@@ -301,7 +302,7 @@
         return dot(leg_in[i], one_hot(hub_lane_ref[...], HUB_LATS)).astype(BF16)
 
     def of_slot(i, j, value):
-        low = degs - wave_at(device(chip - SIDES[i] * reach, core), 0)
+        low = degs - wave_at(device(chip - (1 - 2 * i) * reach, core), 0)
         row = lax.broadcasted_iota(jnp.int32, value.shape, 0)
         return jnp.where((row < low) == (j == 0), value, 0.0)
 
@@ -373,12 +374,12 @@
             )
         scale_v[1:2, :] = gain_ref[...] / jnp.sqrt(scale_v[1:2, :] + 1e-05)
 
-        for i in range(2):
+        def one_side(i, carry):
             to_side(leg_out.at[i], leg_in, leg_sem, i, 1).wait()
             pltpu.make_async_copy(
                 hub_in.at[i, pl.ds(0, served - 1)], hub_in.at[i, pl.ds(0, served - 1)], hub_sem.at[i]
             ).wait()
-            owner = device(chip - SIDES[i] * reach, core)
+            owner = device(chip - (1 - 2 * i) * reach, core)
             arrived = hub_in[i].reshape(served * GROUP, thirds * chans)
             ordered = dot(one_hot(hub_gather_ref[...], 2 * PER_CHUNK * hub_fold), arrived)
             for q in range(2 * PER_CHUNK):
@@ -392,6 +393,9 @@
             total = of_slot(i, 0, dot(leg, hub_spec_v[0])) + of_slot(i, 1, dot(leg, hub_spec_v[1]))
             part_out[i] = total.astype(BF16)
             to_side(part_out.at[i], part_in, part_sem, i, -1).start()
+            return carry
+
+        lax.fori_loop(0, 2, one_side, 0)
 
     scale_v[...] = jnp.zeros_like(scale_v)
     acc_v[...] = jnp.zeros_like(acc_v)
@@ -399,7 +403,7 @@
     build_table(last)
     transform(last)
     loads[2].wait()
-    for i, side in enumerate(SIDES):
+    for i, side in enumerate((1, -1)):
         at_chip = lax.rem(chip + side * hub_chip_ref[...] + 2 * chips, chips)
         lats = one_hot(at_chip * (2 * lat_dev) + hub_inner_ref[i], nlat)
         rows_here = jnp.zeros((packed, HUB_LATS), F32)
@@ -456,11 +460,11 @@
 
     lax.fori_loop(0, slots, prepare, 0)
 
-    table_row = lax.broadcasted_iota(jnp.int32, (2 * degs_kept, rows), 0)
+    table_row = lax.broadcasted_iota(jnp.int32, (2 * degs_kept, rows // HALVES), 0)
     weight = jnp.where((table_row == 0) | (table_row == degs_kept), 1.0, 2.0)
 
     def build_table_t(k, carry):
-        chosen = (chosen_v[k].astype(F32) * weight).astype(BF16)
+        chosen = (dot(chosen_v[k], one_hot(single_ref[...], rows)) * weight).astype(BF16)
         table_t_v[k] = dot_tn(cos_v[...], chosen).astype(BF16)
         return carry
 
@@ -481,7 +485,7 @@
 
         @pl.when(k == 0)
         def _():
-            for i in range(2):
+            def one_side(i, carry):
                 to_side(mix_out, mix_in, mix_sem, i, 1).wait()
                 leg = hub_legendre(i)
                 for j in range(PER_CHUNK):
@@ -496,6 +500,9 @@
                 home = dot(one_hot(hub_scatter_ref[...], served * GROUP), hub_z_v[...])
                 hub_out[i] = home.reshape(served, GROUP, thirds * chans).astype(BF16)
                 send_from_hub(i)
+                return carry
+
+            lax.fori_loop(0, 2, one_side, 0)
 
         @pl.when(k != last)
         def _():
@@ -557,15 +564,12 @@
 
     lax.fori_loop(0, chunks, middle, 0)
 
-    blocks = 10
-    lane_half = (
-        lax.broadcasted_iota(jnp.int32, (rows, thirds * chans), 0) // (GROUP // HALVES) % HALVES
-    )
-
     def take(k):
-        returned = in_two[pl.ds(k * count, count)].reshape(rows, thirds * chans).astype(F32)
+        returned = in_two[pl.ds(k * count, count)].reshape(rows, thirds * chans)
         for h in range(HALVES):
-            masked_v[h] = jnp.where(lane_half == h, returned, 0.0).astype(BF16)
+            picked = dot(one_hot(pick_ref[h], rows // HALVES), returned).astype(BF16)
+            for t in range(thirds):
+                picked_v[h * thirds + t] = picked[:, t * chans : (t + 1) * chans]
 
     def inner(turn, carry):
         k = last - turn
@@ -573,39 +577,41 @@
         pl.when(k != last)(lambda: wait_chunk(k, in_two, recv_two, count - 1))
         take(k)
 
-        def block(i, carry):
-            h = i // blocks
-            at = pl.ds(pl.multiple_of(lax.rem(i, blocks) * part, 16), part)
-            acc_v[h, at, :] += dot(table_t_v[k, at, :], masked_v[h])
+        def plane(a, carry):
+            acc_v[a] += dot(table_t_v[k], picked_v[a])
             return carry
 
-        return lax.fori_loop(0, HALVES * blocks, block, carry)
+        return lax.fori_loop(0, lat_dev, plane, carry)
 
     lax.fori_loop(0, chunks - 1, inner, 0)
     wait_chunk(0, in_two, recv_two, count - 1)
     take(0)
 
-    def last_block(i, carry):
-        h = i // blocks
-        at = pl.ds(pl.multiple_of(lax.rem(i, blocks) * part, 16), part)
-        filtered = (acc_v[h, at, :] + dot(table_t_v[0, at, :], masked_v[h])) * inv_root
-        for t in range(thirds):
-            a = h * thirds + t
-            normed = (
-                (field_v[a, at, :].astype(F32) - scale_v[0:1, :]) * scale_v[1:2, :]
-            ).astype(BF16)
-            field_v[a, at, :] = (
-                normed.astype(F32) + filtered[:, t * chans : (t + 1) * chans]
-            ).astype(BF16)
-        these = pl.ds(h * thirds, thirds)
-        pltpu.make_async_copy(field_v.at[these, at, :], out_hbm.at[these, at, :], store_sem).start()
+    def last_plane(a, carry):
+        filtered = (acc_v[a] + dot(table_t_v[0], picked_v[a])) * inv_root
+        normed = ((field_v[a].astype(F32) - scale_v[0:1, :]) * scale_v[1:2, :]).astype(BF16)
+        field_v[a] = (normed.astype(F32) + filtered).astype(BF16)
+        pltpu.make_async_copy(field_v.at[a], out_hbm.at[a], store_sem).start()
         return carry
 
-    lax.fori_loop(0, HALVES * blocks, last_block, 0)
+    lax.fori_loop(0, lat_dev, last_plane, 0)
     pltpu.make_async_copy(field_v, out_hbm, store_sem).wait()
     for amount in [count - 1] * (2 * last) + [near - 1, 2 * (served - 1)] * 2:
         sent = in_one.at[pl.ds(0, amount)]
         pltpu.make_async_copy(sent, sent, send_sem).wait()
+
+
+def hand_over(src, dst, through, load_sem, store_sem):
+    planes = range(src.shape[0])
+    loads = [pltpu.make_async_copy(src.at[a], through.at[a], load_sem.at[a]) for a in planes]
+    stores = [pltpu.make_async_copy(through.at[a], dst.at[a], store_sem.at[a]) for a in planes]
+    for load in loads:
+        load.start()
+    for load, store in zip(loads, stores):
+        load.wait()
+        store.start()
+    for store in stores:
+        store.wait()
 
 
 def cosine_rows(waves, width):
@@ -684,14 +690,22 @@
     hub_scatter = np.full((1, 2 * PER_CHUNK * hub_fold), -1, np.int32)
     hub_scatter[0, goes] = came
 
+    d, h, q = np.meshgrid(
+        np.arange(count), np.arange(HALVES), np.arange(2 * PER_CHUNK), indexing="ij"
+    )
+    pick = np.full((HALVES, 1, rows), -1, np.int32)
+    pick[h, 0, d * GROUP + h * 2 * PER_CHUNK + q] = d * 2 * PER_CHUNK + q
+    d, q = np.meshgrid(np.arange(count), np.arange(2 * PER_CHUNK), indexing="ij")
+    single = (d * GROUP + q).reshape(1, -1).astype(np.int32)
+
     smem = pl.BlockSpec(memory_space=pltpu.SMEM)
     vmem = pl.BlockSpec(memory_space=pltpu.VMEM)
     hbm = pl.BlockSpec(memory_space=pl.ANY)
     parcels = (chunks * count, GROUP, wide)
-    return pl.pallas_call(
+    result = pl.pallas_call(
         functools.partial(layer_kernel, count, float(lat_dev * count * width)),
         out_shape=jax.ShapeDtypeStruct(field.shape, field.dtype),
-        in_specs=[smem] * 2 + [vmem] * 12 + [hbm] * 4,
+        in_specs=[smem] * 2 + [vmem] * 14 + [hbm] * 4,
         out_specs=hbm,
         scratch_shapes=[
             pltpu.VMEM(field.shape, BF16),
@@ -699,7 +713,7 @@
             pltpu.VMEM(legendre.shape, BF16),
             pltpu.VMEM(mixing.shape, BF16),
             pltpu.VMEM((chunks, rows, width), BF16),
-            pltpu.VMEM((chunks, width, rows), BF16),
+            pltpu.VMEM((chunks, width, rows // HALVES), BF16),
             pltpu.VMEM(parcels, BF16),
             pltpu.VMEM(parcels, BF16),
             pltpu.VMEM(parcels, BF16),
@@ -709,8 +723,8 @@
             pltpu.VMEM((slots, 2 * chans, 2 * chans), BF16),
             pltpu.VMEM((PER_CHUNK, nlat, 2 * chans), BF16),
             pltpu.VMEM((rows, wide), BF16),
-            pltpu.VMEM((HALVES, rows, wide), BF16),
-            pltpu.VMEM((HALVES, width, wide), F32),
+            pltpu.VMEM((lat_dev, rows // HALVES, chans), BF16),
+            pltpu.VMEM((lat_dev, width, chans), F32),
             pltpu.VMEM((chunks, 2 * degs, rows), BF16),
             pltpu.VMEM((2, served, GROUP, wide), BF16),
             pltpu.VMEM((2, served, GROUP, wide), BF16),
@@ -749,7 +763,7 @@
     )(
         slot_wave,
         jnp.asarray(sums),
-        slot_wave[None],
+        slot_wave,
         jnp.asarray(slot),
         jnp.asarray(lat_old),
         jnp.asarray(lat_new),
@@ -760,12 +774,26 @@
         jnp.asarray(hub_lane),
         jnp.asarray(hub_gather),
         jnp.asarray(hub_scatter),
+        jnp.asarray(pick),
+        jnp.asarray(single),
         gain[None],
         field,
         jnp.asarray(cosines),
         legendre,
         mixing,
     )
+    return pl.pallas_call(
+        hand_over,
+        out_shape=jax.ShapeDtypeStruct(field.shape, field.dtype),
+        in_specs=[hbm],
+        out_specs=hbm,
+        scratch_shapes=[
+            pltpu.VMEM(field.shape, BF16),
+            pltpu.SemaphoreType.DMA((lat_dev,)),
+            pltpu.SemaphoreType.DMA((lat_dev,)),
+        ],
+        name="result",
+    )(result)
 
 
 def solution(mesh):

time: 442 us -> 438 us (level)
  local copies, waits for them, and re-layouts: 5.87 us -> 0 us
    unnamed x1 -> x0, local copies, waits for them, and re-layouts: 4.63 us -> none
where the time goes in v5:
time: 438 us; the launch traced here: 437 us
  Pallas kernels  437 us (100%)
    pallas_call x1, Pallas kernels, per_device(): pl.pallas_call(functools.partial(layer_kernel, count, float(lat_dev * cou...  434 us

profile of v5, /device:TPU:37, one launch (start us, length us, event | category | flops | bytes accessed | tf_op | source)
XLA Modules:
  0.0 437.4 jit_solution(13478151816369649507)
XLA Ops:
  0.0 433.7 %layer.1.src = bf16[6,1440,256]{2,1,0:T(8,128)(2,1)} custom-call(s32[384]{0:T(512)} %wave_row_ref.1, f32[768]{0:T(1024)} %constant.28.clone.rowsum_ref, s32[384]{0:T(512)} %wave_row_ref.1, s32[3,2,1,512]{3,2,1,0:T(1,128)} %constant.29.clone.slot_ref, s32[1,384]{1,0:T(1,128)} %constant.30.clone.lat_old_ref, s32[1,384]{1,0:T(1,128)} %constant.31.clone.lat_new_ref, ...), custom_call_target="tpu_custom_call" | custom-call | tf_op jit(solution)/shard_map/layer/pallas_call | solution.py:705
  433.8 3.7 result.1

commit v6 on v5

--- a/solution.py
+++ b/solution.py
@@ -398,10 +398,29 @@
         lax.fori_loop(0, 2, one_side, 0)
 
     scale_v[...] = jnp.zeros_like(scale_v)
-    acc_v[...] = jnp.zeros_like(acc_v)
 
     build_table(last)
     transform(last)
+    pl.semaphore_wait(barrier, count - 1)
+
+    pair = tell(mine_v, other_v, 0, partner)
+    pair.start()
+    send_to_hubs()
+    send_near(out_one, in_one, recv_one)
+    in_one[last * count + me] = out_one[last * count + me]
+    pair.wait()
+    gap = mine_v[0:1, :] - other_v[0:1, :]
+    pair_mean = (mine_v[0:1, :] + other_v[0:1, :]) * 0.5
+    pair_squares = mine_v[1:2, :] + other_v[1:2, :] + (0.5 * local_count) * gap * gap
+    half_v[0:1, :] = jnp.where(core == 0, pair_mean[:, :lanes], pair_mean[:, lanes:])
+    half_v[1:2, :] = jnp.where(core == 0, pair_squares[:, :lanes], pair_squares[:, lanes:])
+    halves_v[me // 2] = half_v[...]
+
+    def send_stats(i, carry):
+        tell(half_v, halves_v.at[me // 2], 2, lax.rem(me + 2 * i, count)).start()
+        return carry
+
+    lax.fori_loop(1, count // 2, send_stats, 0)
     loads[2].wait()
     for i, side in enumerate((1, -1)):
         at_chip = lax.rem(chip + side * hub_chip_ref[...] + 2 * chips, chips)
@@ -411,28 +430,8 @@
             values = dot(legendre_v[last * PER_CHUNK + j], lats).astype(BF16)
             rows_here += dot_tn(pack(me, j), values)
         leg_out[i] = rows_here.astype(BF16)
-    pl.semaphore_wait(barrier, count - 1)
-
-    pair = tell(mine_v, other_v, 0, partner)
-    pair.start()
-    pair.wait()
-    gap = mine_v[0:1, :] - other_v[0:1, :]
-    pair_mean = (mine_v[0:1, :] + other_v[0:1, :]) * 0.5
-    pair_squares = mine_v[1:2, :] + other_v[1:2, :] + (0.5 * local_count) * gap * gap
-    half_v[0:1, :] = jnp.where(core == 0, pair_mean[:, :lanes], pair_mean[:, lanes:])
-    half_v[1:2, :] = jnp.where(core == 0, pair_squares[:, :lanes], pair_squares[:, lanes:])
-    halves_v[me // 2] = half_v[...]
-
-    def send_stats(i, carry):
-        tell(half_v, halves_v.at[me // 2], 2, lax.rem(me + 2 * i, count)).start()
-        return carry
-
-    lax.fori_loop(1, count // 2, send_stats, 0)
     for i in range(2):
         to_side(leg_out.at[i], leg_in, leg_sem, i, 1).start()
-    send_to_hubs()
-    send_near(out_one, in_one, recv_one)
-    in_one[last * count + me] = out_one[last * count + me]
 
     def outward(turn, carry):
         k = last - turn
@@ -444,6 +443,7 @@
         return carry
 
     lax.fori_loop(1, chunks, outward, 0)
+    acc_v[...] = jnp.zeros_like(acc_v)
 
     loads[3].wait()
 

time: 438 us -> 435 us (level); the launches traced: 437 us -> 428 us
  Pallas kernels: 437 us -> 428 us
    pallas_call x1, Pallas kernels: 434 us -> 424 us  [per_device(): pl.pallas_call(functools.partial(layer_kernel, count, float(lat_dev * cou...]
where the time goes in v6:
time: 435 us; the launch traced here: 428 us
  Pallas kernels  428 us (98%)
    pallas_call x1, Pallas kernels, per_device(): pl.pallas_call(functools.partial(layer_kernel, count, float(lat_dev * cou...  424 us

profile of v6, /device:TPU:37, one launch (start us, length us, event | category | flops | bytes accessed | tf_op | source)
XLA Modules:
  0.0 428.1 jit_solution(2461353925424655280)
XLA Ops:
  0.0 424.4 %layer.1.src = bf16[6,1440,256]{2,1,0:T(8,128)(2,1)} custom-call(s32[384]{0:T(512)} %wave_row_ref.1, f32[768]{0:T(1024)} %constant.28.clone.rowsum_ref, s32[384]{0:T(512)} %wave_row_ref.1, s32[3,2,1,512]{3,2,1,0:T(1,128)} %constant.29.clone.slot_ref, s32[1,384]{1,0:T(1,128)} %constant.30.clone.lat_old_ref, s32[1,384]{1,0:T(1,128)} %constant.31.clone.lat_new_ref, ...), custom_call_target="tpu_custom_call" | custom-call | tf_op jit(solution)/shard_map/layer/pallas_call | solution.py:705
  424.4 3.7 result.1
